TPU v7x, 32 devices: a whole 2x2x4 slice. The times are simulated.
32 devices in a mesh: group: 4 (over x, core), tile: 8 (over z, y).
Axes of the slice: x: 2, y: 2, z: 4, core: 2. Of those that a mesh axis runs over, the one named last changes fastest.
Arguments:
- tokens: bfloat16 [64, 256, 128], P('group', 'tile'), may hold values from -6 to 6
- gain1: float32 [128], replicated, may hold values from 0.25 to 1.75
- w_qkv: bfloat16 [128, 384], replicated, may hold values from -0.5 to 0.5
- w_proj: bfloat16 [128, 128], replicated, may hold values from -0.5 to 0.5
- bias_table: float32 [4, 31, 31], replicated, may hold values from -70 to 150
- gain2: float32 [128], replicated, may hold values from 0.25 to 1.75
- w_fc1: bfloat16 [128, 512], replicated, may hold values from -0.5 to 0.5
- w_fc2: bfloat16 [512, 128], replicated, may hold values from -0.25 to 0.25
- cotangent: bfloat16 [64, 256, 128], P('group', 'tile'), may hold values from -6 to 6
Outputs:
- block_output: bfloat16 [64, 256, 128], P('group', 'tile')
- grad_tokens: bfloat16 [64, 256, 128], P('group', 'tile')
- grad_gain1: float32 [128], replicated
- grad_qkv: float32 [128, 384], replicated
- grad_proj: float32 [128, 128], replicated
- grad_table: float32 [4, 31, 31], replicated
- grad_gain2: float32 [128], replicated
- grad_fc1: float32 [128, 512], replicated
- grad_fc2: float32 [512, 128], replicated
All inputs are finite; a program needn't handle non-finite values.
Results may differ from a plain program's by a relative error of at most 0.019.
Values may be sent and summed in bfloat16 or wider, within the bound.
No kernel may reach another device: no remote copies, remote signals or barrier semaphores. Data moves between devices by JAX's collectives and lax.ppermute only.
A program may use at most 64 MiB of HBM per device.

v0:
```python
import functools
import math

import jax
import jax.numpy as jnp
from jax import lax
from jax.experimental import pallas as pl
from jax.experimental.pallas import tpu as pltpu
from jax.sharding import PartitionSpec as P


WIN = 16
SHIFT = 8
NORM_EPS = 1e-05
LOG2_E = math.log2(math.e)
LANES = 128
F32 = jnp.float32
BF16 = jnp.bfloat16
AXES = ("group", "tile")
PARAMS = pltpu.CompilerParams(vmem_limit_bytes=24 * 1024 * 1024)


def dot(left, right, left_dim, right_dim, precision=None):
    return lax.dot_general(
        left,
        right,
        (((left_dim,), (right_dim,)), ((), ())),
        preferred_element_type=F32,
        precision=precision,
    )


def iota(shape, dim):
    return lax.broadcasted_iota(jnp.int32, shape, dim)


def shift_rows(values, amounts, right):
    width = values.shape[1]
    for bit in range(4):
        step = 1 << bit
        moved = pltpu.roll(values, step if right else width - step, 1)
        values = jnp.where((amounts & step) != 0, moved, values)
    return values


def bias_kernel(heads, windows, table_ref, out_ref, pad_ref):
    span = 2 * WIN * WIN
    tokens = WIN * WIN
    offsets = 2 * WIN - 1
    block = offsets + 1
    pad_ref[...] = jnp.zeros_like(pad_ref)
    for head in range(heads):
        pad_ref[head * block : head * block + offsets, :offsets] = table_ref[:, head, :]
    padded = pad_ref[...]
    parts = []
    for _ in range(3):
        part = padded.astype(BF16)
        parts.append(part)
        padded = padded - part.astype(F32)
    chosen = iota((LANES, span), 1) % 32 == offsets - 1 - iota((LANES, span), 0)
    spread = dot(jnp.concatenate(parts, 0), jnp.where(chosen, 1.0, 0.0).astype(BF16), 1, 0)
    size = heads * block
    spread = spread[:size] + spread[size : 2 * size] + spread[2 * size :]
    flats = []
    for odd in range(2):
        wanted = offsets - 1 - iota((block, span), 0)
        keep = (iota((block, span), 1) // 32) * 2 + odd == wanted
        for head in range(heads):
            mine = spread[head * block : (head + 1) * block]
            flat = jnp.sum(jnp.where(keep, mine, 0.0), axis=0, keepdims=True)
            flats.append(jnp.broadcast_to(flat, (WIN, span)))
    rows = heads * WIN
    amounts = WIN - 1 - iota((rows, span), 0) % WIN
    even = shift_rows(jnp.concatenate(flats[:heads], 0), amounts, False)
    odd = shift_rows(jnp.concatenate(flats[heads:], 0), amounts, False)
    odd = pltpu.roll(odd, WIN, 1)
    strip = jnp.where(iota((rows, span), 1) % 32 < WIN, even, odd) * LOG2_E
    last_row = (lax.axis_index("group") == 0).astype(jnp.int32)
    last_col = (lax.axis_index("tile") == 0).astype(jnp.int32)
    key = iota((WIN, tokens), 1)
    query_x = iota((WIN, tokens), 0)
    key_low = (key >= tokens // 2).astype(jnp.int32)
    cross_col = ((key % WIN >= SHIFT) != (query_x >= SHIFT)).astype(jnp.int32)
    for fine in range(8):
        moved = pltpu.roll(strip, (span - WIN * fine) % span, 1)
        for coarse in range(2):
            y = WIN - 1 - (8 * coarse + fine)
            cross_row = key_low if y < SHIFT else 1 - key_low
            for window in range(windows):
                apart = cross_row * last_row
                if window == windows - 1:
                    apart = apart + cross_col * last_col
                extra = jnp.where(apart > 0, -1e30, 0.0)
                for head in range(heads):
                    part = moved[
                        head * WIN : (head + 1) * WIN,
                        LANES * coarse : LANES * coarse + tokens,
                    ]
                    start = head * tokens + y * WIN
                    out_ref[window, start : start + WIN, :] = part + extra


def mean_of(values):
    return jnp.mean(values, axis=-1, keepdims=True)


def norm(values):
    centred = values - mean_of(values)
    scale = lax.rsqrt(mean_of(centred * centred) + NORM_EPS)
    return centred * scale, scale


def norm_back(grad, unit, scale):
    return scale * (grad - mean_of(grad) - unit * mean_of(grad * unit))


def cut_kernel(token_ref, cot_ref, table_ref, below_ref, right_ref, diag_ref, table_out, sems):
    copies = []

    def copy(source, target):
        copies.append(pltpu.make_async_copy(source, target, sems.at[len(copies)]))

    keep = token_ref.shape[1] - SHIFT
    high, low = pl.ds(0, SHIFT), pl.ds(SHIFT, SHIFT)
    most, rest = pl.ds(0, keep), pl.ds(keep, SHIFT)
    for index, tile_ref in enumerate((token_ref, cot_ref)):
        copy(tile_ref.at[low, most], below_ref.at[index])
        copy(tile_ref.at[high, rest], right_ref.at[index])
        copy(tile_ref.at[low, rest], diag_ref.at[index])
    copy(table_ref, table_out)
    for each in copies:
        each.start()
    for each in copies:
        each.wait()


def block_kernel(heads, first, count, last, *refs):
    token_ref, cot_ref, below_ref = refs[:3]
    refs = refs[3:]
    if last:
        right_ref, diag_ref, sums_in, strip_in, gains_in = refs[:5]
        refs = refs[5:]
    bias_ref, gain1_ref, qkv_ref, proj_ref, gain2_ref, fc1_ref, fc2_ref = refs[:7]
    own_out, below_out = refs[7:9]
    refs = refs[9:]
    if last:
        right_out, diag_out, keep_out, send_out, grads_ref = refs[:5]
        refs = refs[5:]
    else:
        sums_out, strip_out, gains_out = refs[:3]
        refs = refs[3:]
    x_ref, c_ref, n_ref, unit_ref, scale_ref, q_ref, k_ref, v_ref = refs[:8]
    p_ref, att_ref, out_f32_ref, inverse_ref, dh_ref, dqkv_ref, ds_ref, dsn_ref = refs[8:16]
    inner_ref, before_ref, out_ref = refs[16:]

    tokens = WIN * WIN
    width = token_ref.shape[2]
    head_size = width // heads
    hidden_units = fc1_ref.shape[1]

    def put(row, value):
        rows = slice(row, row + value.shape[0])
        if last:
            grads_ref[rows, :] = (sums_in[rows, :] + value).astype(BF16)
        else:
            sums_out[rows, :] = value

    def assemble(tile_ref, index, target):
        tile = tile_ref[...].astype(F32)
        above = below_ref[index].astype(F32)
        for window in range(count):
            cols = slice(WIN * (first + window) + SHIFT, WIN * (first + window) + SHIFT + WIN)
            if last and window == count - 1:
                left = right_ref[index].astype(F32)
                diag = diag_ref[index].astype(F32)
                top = jnp.concatenate([diag, above[:, :SHIFT]], 1)
                low = jnp.concatenate([left, tile[:SHIFT, :SHIFT]], 1)
            else:
                top = above[:, cols]
                low = tile[:SHIFT, cols]
            both = jnp.concatenate([top, low], 0).reshape(tokens, width)
            target[window * tokens : (window + 1) * tokens, :] = both.astype(target.dtype)

    assemble(token_ref, 0, x_ref)
    assemble(cot_ref, 1, c_ref)

    unit1, scale1 = norm(x_ref[...])
    unit_ref[...] = unit1
    scale_ref[...] = scale1
    normed = (unit1 * gain1_ref[...]).astype(BF16)
    n_ref[...] = normed
    projected = dot(normed, qkv_ref[...], 1, 0)
    q_ref[...] = projected[:, :width]
    k_ref[...] = projected[:, width : 2 * width].astype(BF16)
    v_ref[...] = projected[:, 2 * width :].astype(BF16)
    lane_head = iota((1, width), 1) // head_size
    score_scale = head_size ** (-0.5)

    def of_head(values, head):
        return jnp.where(lane_head == head, values, 0.0).astype(BF16)

    for window in range(count):
        span = slice(window * tokens, (window + 1) * tokens)
        query = q_ref[span, :]
        keys = k_ref[span, :]
        value = v_ref[span, :].astype(F32)
        sources = []
        for head in range(heads):
            scores = dot(of_head(query, head), keys, 1, 1) * (score_scale * LOG2_E)
            scores = scores + bias_ref[first + window, head * tokens : (head + 1) * tokens, :]
            weights = jnp.exp2(scores - jnp.max(scores, axis=-1, keepdims=True))
            p_ref[window, :, head * tokens : (head + 1) * tokens] = weights.astype(BF16)
            ones = jnp.broadcast_to(of_head(jnp.ones((1, width), F32), head), (tokens, width))
            sources.append(jnp.concatenate([of_head(value, head), ones], 1))
        both = dot(p_ref[window], jnp.concatenate(sources, 0), 1, 0)
        inverse = 1.0 / both[:, width:]
        attended = both[:, :width] * inverse
        inverse_ref[span, :] = inverse
        out_f32_ref[span, :] = attended
        att_ref[span, :] = attended.astype(BF16)

    hidden = x_ref[...] + dot(att_ref[...], proj_ref[...], 1, 0).astype(BF16).astype(F32)
    unit2, scale2 = norm(hidden)
    normed2 = (unit2 * gain2_ref[...]).astype(BF16)
    cot = c_ref[...]
    root = math.sqrt(0.5)
    step = 2 * width
    for part in range(hidden_units // step):
        cols = slice(part * step, (part + 1) * step)
        before = dot(normed2, fc1_ref[:, cols], 1, 0)
        normal = 0.5 * (1.0 + lax.erf(before * root))
        inner_ref[:, cols] = (before * normal).astype(BF16)
        density = jnp.exp2(before * before * (-0.5 * LOG2_E)) * (1.0 / math.sqrt(2.0 * math.pi))
        slope = normal + before * density
        grad_inner = dot(cot, fc2_ref[cols, :], 1, 1).astype(BF16).astype(F32)
        before_ref[:, cols] = (grad_inner * slope).astype(BF16)
    inner = inner_ref[...]
    grad_before = before_ref[...]
    out_ref[...] = hidden + dot(inner, fc2_ref[...], 1, 0)
    back = dot(grad_before, fc1_ref[...], 1, 1).astype(BF16).astype(F32)
    grad_fc1 = dot(normed2, grad_before, 0, 0)
    for part in range(hidden_units // width):
        put(part * width, grad_fc1[:, part * width : (part + 1) * width])
    put(hidden_units, dot(inner, cot, 0, 0))
    grad_gain2 = jnp.sum(back * unit2, axis=0, keepdims=True)
    grad_hidden = cot.astype(F32) + norm_back(back * gain2_ref[...], unit2, scale2)
    dh_ref[...] = grad_hidden

    grad_attended = grad_hidden.astype(BF16)
    put(2 * hidden_units + 3 * width, dot(att_ref[...], grad_attended, 0, 0))
    grad_heads = dot(grad_attended, proj_ref[...], 1, 1).astype(BF16).astype(F32)

    minus = jnp.full((tokens, width), -1.0, BF16)
    for window in range(count):
        span = slice(window * tokens, (window + 1) * tokens)
        query = q_ref[span, :]
        keys = k_ref[span, :].astype(F32)
        value = jnp.concatenate([v_ref[span, :], minus], 1)
        scaled = (grad_heads[span, :] * inverse_ref[span, :]).astype(BF16).astype(F32)
        inside = scaled * out_f32_ref[span, :]
        inside_high = inside.astype(BF16).astype(F32)
        inside_low = pltpu.roll(inside - inside_high, head_size, 1)
        query_t = query.T.astype(BF16)
        scaled_t = scaled.T.astype(BF16)
        grad_k, grad_v, sources = [], [], []
        for head in range(heads):
            rows = slice(head * tokens, (head + 1) * tokens)
            part = slice(head * head_size, (head + 1) * head_size)
            extra = jnp.where(
                lane_head == head,
                inside_high,
                jnp.where(lane_head == (head + 1) % heads, inside_low, 0.0),
            ).astype(BF16)
            grad_weights = dot(jnp.concatenate([of_head(scaled, head), extra], 1), value, 1, 1)
            weights = p_ref[window, :, rows]
            grad_scores = grad_weights * weights.astype(F32)
            if window == 0:
                ds_ref[rows, :] = grad_scores
            else:
                ds_ref[rows, :] += grad_scores
            narrow = grad_scores.astype(BF16)
            dsn_ref[:, rows] = narrow
            sources.append(of_head(keys, head))
            grad_k.append(dot(query_t[part, :], narrow, 1, 0))
            grad_v.append(dot(scaled_t[part, :], weights, 1, 0))
        grad_q = dot(dsn_ref[...], jnp.concatenate(sources, 0), 1, 0)
        dqkv_ref[span, :width] = (grad_q * score_scale).astype(BF16)
        grad_k = jnp.concatenate(grad_k, 0).T
        dqkv_ref[span, width : 2 * width] = (grad_k * score_scale).astype(BF16)
        dqkv_ref[span, 2 * width :] = jnp.concatenate(grad_v, 0).T.astype(BF16)

    grad_projected = dqkv_ref[...]
    grad_qkv = dot(n_ref[...], grad_projected, 0, 0)
    for part in range(3):
        put(2 * hidden_units + part * width, grad_qkv[:, part * width : (part + 1) * width])
    grad_normed = dot(grad_projected, qkv_ref[...], 1, 1).astype(BF16).astype(F32)
    unit1 = unit_ref[...]
    grad_gain1 = jnp.sum(grad_normed * unit1, axis=0, keepdims=True)
    grad_x = dh_ref[...] + norm_back(grad_normed * gain1_ref[...], unit1, scale_ref[...])
    gains = jnp.concatenate([grad_gain1, grad_gain2, jnp.zeros((6, width), F32)], 0)

    lanes = 2 * tokens
    rows = heads * WIN
    blank = jnp.zeros((WIN, LANES), F32)
    strip = strip_in[...] if last else jnp.zeros((rows, lanes), F32)
    for fine in range(8):
        near, far = WIN - 1 - fine, WIN - 9 - fine
        blocks = []
        for head in range(heads):
            above = ds_ref[head * tokens + near * WIN : head * tokens + (near + 1) * WIN, :]
            under = ds_ref[head * tokens + far * WIN : head * tokens + (far + 1) * WIN, :]
            blocks.append(
                jnp.concatenate([above, blank, blank], 1) + jnp.concatenate([blank, under, blank], 1)
            )
        block = jnp.concatenate(blocks, 0)
        strip = strip + (pltpu.roll(block, WIN * fine, 1) if fine else block)

    if last:
        finish_table(heads, strip, grads_ref, 2 * hidden_units + 4 * width)
        row = 2 * hidden_units + 4 * width + heads * 2 * WIN
        blank = jnp.zeros((grads_ref.shape[0] - row - 8, width), F32)
        grads_ref[row:, :] = jnp.concatenate([gains_in[...] + gains, blank], 0).astype(BF16)
        half = keep_out.shape[0]
        core = lax.axis_index("group") % 2
        keep_out[...] = grads_ref[pl.ds(pl.multiple_of(core * half, 16), half), :]
        send_out[...] = grads_ref[pl.ds(pl.multiple_of((1 - core) * half, 16), half), :]
    else:
        strip_out[...] = strip
        gains_out[...] = gains

    for index, values in enumerate((out_ref[...], grad_x)):
        for window in range(count):
            start = WIN * window
            block = values[window * tokens : (window + 1) * tokens, :].reshape(WIN, WIN, width)
            top, low = block[:SHIFT], block[SHIFT:]
            if last and window == count - 1:
                own_out[index, :, start:, :] = low[:, SHIFT:].astype(BF16)
                below_out[index, :, start:, :] = top[:, SHIFT:].astype(BF16)
                right_out[index] = low[:, :SHIFT].astype(BF16)
                diag_out[index] = top[:, :SHIFT].astype(BF16)
            else:
                own_out[index, :, start : start + WIN, :] = low.astype(BF16)
                below_out[index, :, start : start + WIN, :] = top.astype(BF16)


def finish_table(heads, strip, grads_ref, row):
    rows, lanes = strip.shape
    lane = iota((rows, lanes), 1)
    amounts = WIN - 1 - iota((rows, lanes), 0) % WIN
    offsets = 2 * WIN
    table = jnp.zeros((heads * offsets, LANES), F32)
    for odd in range(2):
        chosen = jnp.where((lane // WIN) % 2 == odd, strip, 0.0)
        if odd:
            chosen = pltpu.roll(chosen, lanes - WIN, 1)
        chosen = shift_rows(chosen, amounts, True)
        wanted = offsets - 2 - iota((offsets, lanes), 0)
        where_row = (iota((offsets, lanes), 1) // 32) * 2 + odd == wanted
        terms = []
        for head in range(heads):
            flat = jnp.sum(chosen[head * WIN : (head + 1) * WIN, :], axis=0, keepdims=True)
            terms.append(jnp.where(where_row, flat, 0.0))
        terms = jnp.concatenate(terms, 0).astype(BF16)
        pick_lane = iota((lanes, LANES), 0) % 32
        pick = jnp.where(pick_lane == offsets - 2 - iota((lanes, LANES), 1), 1.0, 0.0).astype(BF16)
        table = table + dot(terms, pick, 1, 0)
    grads_ref[row : row + heads * offsets, :] = table.astype(BF16)


def pair_kernel(first_ref, second_ref, out_ref):
    total = first_ref[...].astype(F32) + second_ref[...].astype(F32)
    out_ref[...] = total.astype(out_ref.dtype)


def sum_kernel(in_ref, out_ref):
    total = in_ref[0].astype(F32)
    for index in range(1, in_ref.shape[0]):
        total = total + in_ref[index].astype(F32)
    total = total.astype(out_ref.dtype)
    for index in range(out_ref.shape[0]):
        out_ref[index] = total


def unpack_kernel(
    heads,
    factor,
    mine_ref,
    other_ref,
    diag_ref,
    above_first_ref,
    above_last_ref,
    left_ref,
    own_first_ref,
    own_last_ref,
    out_ref,
    grad_ref,
    gain1_ref,
    qkv_ref,
    proj_ref,
    table_ref,
    gain2_ref,
    fc1_ref,
    fc2_ref,
    summed_ref,
):
    width, hidden_units = fc1_ref.shape
    half = mine_ref.shape[0]
    early = own_first_ref.shape[2]
    for index, target in enumerate((out_ref, grad_ref)):
        target[:SHIFT, :SHIFT, :] = own_last_ref[index]
        target[:SHIFT, SHIFT : SHIFT + early, :] = own_first_ref[index]
        target[:SHIFT, SHIFT + early :, :] = left_ref[index]
        target[SHIFT:, :SHIFT, :] = above_last_ref[index]
        target[SHIFT:, SHIFT : SHIFT + early, :] = above_first_ref[index]
        target[SHIFT:, SHIFT + early :, :] = diag_ref[index]
    core = lax.axis_index("group") % 2
    summed_ref[pl.ds(pl.multiple_of(core * half, 16), half), :] = mine_ref[...]
    summed_ref[pl.ds(pl.multiple_of((1 - core) * half, 16), half), :] = other_ref[...]
    offsets = 2 * WIN

    def rows(start, count):
        return summed_ref[start : start + count, :].astype(F32) * factor

    for part in range(hidden_units // width):
        fc1_ref[:, part * width : (part + 1) * width] = rows(part * width, width)
    fc2_ref[...] = rows(hidden_units, hidden_units)
    for part in range(3):
        qkv_ref[:, part * width : (part + 1) * width] = rows(2 * hidden_units + part * width, width)
    start = 2 * hidden_units + 3 * width
    proj_ref[...] = rows(start, width)
    start = start + width
    for head in range(heads):
        block = rows(start + head * offsets, offsets)
        table_ref[:, head, :] = block[: offsets - 1, : offsets - 1]
    start = start + heads * offsets
    gains = rows(start, 16)
    gain1_ref[...] = gains[0:1]
    gain2_ref[...] = gains[1:2]


def neighbour_pairs(row_step, col_step):
    groups, tiles = lax.axis_size("group"), lax.axis_size("tile")
    pairs = []
    for group in range(groups):
        for tile in range(tiles):
            target = ((group + row_step) % groups) * tiles + (tile + col_step) % tiles
            pairs.append((group * tiles + tile, target))
    return pairs


def passed_along(value, row_step, col_step):
    return lax.ppermute(value, AXES, neighbour_pairs(row_step, col_step))


def shards(tokens, gain1, w_qkv, w_proj, bias_table, gain2, w_fc1, w_fc2, cotangent):
    row_count, col_count, width = tokens.shape
    heads = bias_table.shape[0]
    hidden_units = w_fc1.shape[1]
    groups, tiles = lax.axis_size("group"), lax.axis_size("tile")
    devices = groups * tiles
    windows = col_count // WIN
    token_count = WIN * WIN
    keep = col_count - SHIFT

    vmem = pl.BlockSpec(memory_space=pltpu.VMEM)

    def array(shape, dtype=BF16):
        return jax.ShapeDtypeStruct(shape, dtype)

    table = bias_table.transpose(1, 0, 2)
    hbm = pl.BlockSpec(memory_space=pltpu.HBM)
    below, right, diag, table = pl.pallas_call(
        cut_kernel,
        out_shape=(
            array((2, SHIFT, keep, width)),
            array((2, SHIFT, SHIFT, width)),
            array((2, SHIFT, SHIFT, width)),
            array(table.shape, F32),
        ),
        in_specs=[hbm] * 3,
        out_specs=(vmem,) * 4,
        scratch_shapes=[pltpu.SemaphoreType.DMA((7,))],
        name="cut",
        compiler_params=PARAMS,
    )(*(pltpu.with_memory_space_constraint(each, pltpu.HBM) for each in (tokens, cotangent, table)))
    below = passed_along(below, 1, 0)
    right = passed_along(right, 0, 1)
    diag = passed_along(diag, 1, 1)

    bias = pl.pallas_call(
        functools.partial(bias_kernel, heads, windows),
        out_shape=jax.ShapeDtypeStruct((windows, heads * token_count, token_count), F32),
        in_specs=[vmem],
        out_specs=vmem,
        scratch_shapes=[pltpu.VMEM((heads * 2 * WIN, LANES), F32)],
        name="bias",
        compiler_params=PARAMS,
        cost_estimate=pl.CostEstimate(flops=8_000_000, bytes_accessed=2_000_000, transcendentals=0),
    )(table)

    used = 2 * hidden_units + 4 * width + heads * 2 * WIN + 16
    members = devices // 2
    chunk = (used + devices * 8 - 1) // (devices * 8) * 8
    half = chunk * members
    weights = (gain1.reshape(1, width), w_qkv, w_proj, gain2.reshape(1, width), w_fc1, w_fc2)
    sum_rows = 2 * hidden_units + 4 * width

    def block(first, count, last, inputs, outputs):
        total = count * token_count
        scratch = [
            pltpu.VMEM((total, width), F32),
            pltpu.VMEM((total, width), BF16),
            pltpu.VMEM((total, width), BF16),
            pltpu.VMEM((total, width), F32),
            pltpu.VMEM((total, 1), F32),
            pltpu.VMEM((total, width), F32),
            pltpu.VMEM((total, width), BF16),
            pltpu.VMEM((total, width), BF16),
            pltpu.VMEM((count, token_count, heads * token_count), BF16),
            pltpu.VMEM((total, width), BF16),
            pltpu.VMEM((total, width), F32),
            pltpu.VMEM((total, width), F32),
            pltpu.VMEM((total, width), F32),
            pltpu.VMEM((total, 3 * width), BF16),
            pltpu.VMEM((heads * token_count, token_count), F32),
            pltpu.VMEM((token_count, heads * token_count), BF16),
            pltpu.VMEM((total, hidden_units), BF16),
            pltpu.VMEM((total, hidden_units), BF16),
            pltpu.VMEM((total, width), F32),
        ]
        if last:
            scratch = [pltpu.VMEM((2 * half, width), BF16)] + scratch
        inputs = inputs + (bias,) + weights
        return pl.pallas_call(
            functools.partial(block_kernel, heads, first, count, last),
            out_shape=outputs,
            in_specs=[vmem] * len(inputs),
            out_specs=(vmem,) * len(outputs),
            scratch_shapes=scratch,
            name="last" if last else "first",
            compiler_params=PARAMS,
            cost_estimate=pl.CostEstimate(
                flops=1_000_000_000 * count, bytes_accessed=2_000_000, transcendentals=1_000_000
            ),
        )(*inputs)

    early = WIN * (windows - 1)
    own_first, below_first, sums, strip, gains = block(
        0,
        windows - 1,
        False,
        (tokens, cotangent, below),
        (
            array((2, SHIFT, early, width)),
            array((2, SHIFT, early, width)),
            array((sum_rows, width), F32),
            array((heads * WIN, 2 * token_count), F32),
            array((8, width), F32),
        ),
    )
    back_first = passed_along(below_first, -1, 0)
    own_last, below_last, right_last, diag_last, kept, sent = block(
        windows - 1,
        1,
        True,
        (tokens, cotangent, below, right, diag, sums, strip, gains),
        (
            array((2, SHIFT, SHIFT, width)),
            array((2, SHIFT, SHIFT, width)),
            array((2, SHIFT, SHIFT, width)),
            array((2, SHIFT, SHIFT, width)),
            array((half, width)),
            array((half, width)),
        ),
    )
    back_right = passed_along(right_last, 0, -1)
    back_diag = passed_along(diag_last, -1, -1)
    back_below = passed_along(below_last, -1, 0)

    pairs = [(index, index + tiles if index // tiles % 2 == 0 else index - tiles) for index in range(devices)]
    same_core = [
        [index for index in range(devices) if index // tiles % 2 == core] for core in range(2)
    ]

    def exchanged(value):
        return lax.all_to_all(value, AXES, 0, 0, tiled=True, axis_index_groups=same_core)

    received = lax.ppermute(sent, AXES, pairs)
    paired = pl.pallas_call(
        pair_kernel,
        out_shape=jax.ShapeDtypeStruct((half, width), BF16),
        in_specs=[vmem] * 2,
        out_specs=vmem,
        name="pair",
        compiler_params=PARAMS,
    )(kept, received)
    copies = pl.pallas_call(
        sum_kernel,
        out_shape=jax.ShapeDtypeStruct((members, chunk, width), BF16),
        in_specs=[vmem],
        out_specs=vmem,
        name="add",
        compiler_params=PARAMS,
    )(exchanged(paired.reshape(members, chunk, width)))
    mine = exchanged(copies).reshape(half, width)
    other = lax.ppermute(mine, AXES, pairs)

    factor = 1.0 / math.sqrt(row_count * groups * col_count * tiles)
    (
        block_output,
        grad_tokens,
        grad_gain1,
        grad_qkv,
        grad_proj,
        grad_table,
        grad_gain2,
        grad_fc1,
        grad_fc2,
    ) = pl.pallas_call(
        functools.partial(unpack_kernel, heads, factor),
        out_shape=(
            array(tokens.shape),
            array(tokens.shape),
            jax.ShapeDtypeStruct((1, width), F32),
            jax.ShapeDtypeStruct(w_qkv.shape, F32),
            jax.ShapeDtypeStruct(w_proj.shape, F32),
            jax.ShapeDtypeStruct((bias_table.shape[1], heads, bias_table.shape[2]), F32),
            jax.ShapeDtypeStruct((1, width), F32),
            jax.ShapeDtypeStruct(w_fc1.shape, F32),
            jax.ShapeDtypeStruct(w_fc2.shape, F32),
        ),
        in_specs=[vmem] * 8,
        out_specs=(vmem,) * 9,
        scratch_shapes=[pltpu.VMEM((2 * half, width), BF16)],
        name="unpack",
        compiler_params=PARAMS,
    )(mine, other, back_diag, back_first, back_below, back_right, own_first, own_last)

    return (
        block_output,
        grad_tokens,
        grad_gain1.reshape(width),
        grad_qkv,
        grad_proj,
        grad_table.transpose(1, 0, 2),
        grad_gain2.reshape(width),
        grad_fc1,
        grad_fc2,
    )


def solution(mesh):
    tile_spec = P("group", "tile", None)
    return jax.shard_map(
        shards,
        mesh=mesh,
        in_specs=(tile_spec, P(), P(), P(), P(), P(), P(), P(), tile_spec),
        out_specs=(tile_spec, tile_spec, P(), P(), P(), P(), P(), P(), P()),
        check_vma=False,
    )
```

profile of v0, /device:TPU:0, one launch (start us, length us, event | category | flops | bytes accessed | tf_op | source)
XLA Modules:
  0.0 52.8 jit_solution(9816486545119066539)
XLA Ops:
  0.6 0.0 copy-start.1
  0.7 0.0 copy-start
  0.7 0.0 copy-start.3
  0.7 0.0 copy-start.2
  0.7 0.0 copy-start.5
  0.7 0.0 copy-start.4
  0.7 1.1 %cut.1 = (bf16[2,8,24,128]{3,2,1,0:T(8,128)(2,1)S(1)}, bf16[2,8,8,128]{3,2,1,0:T(8,128)(2,1)S(1)}, bf16[2,8,8,128]{3,2,1,0:T(8,128)(2,1)S(1)}, f32[31,4,31]{2,1,0:T(4,128)S(1)}) custom-call(bf16[16,32,128]{2,1,0:T(8,128)(2,1)} %refs_0_.3, bf16[16,32,128]{2,1,0:T(8,128)(2,1)} %refs_1_.3, f32[31,4,31]{2,1,0:T(4,128)} %bitcast.15), custom_call_target="tpu_custom_call" | custom-call | tf_op jit(solution)/shard_map/cut/pallas_call | solution.py:472
  1.8 0.5 %collective-permute-start = (bf16[2,8,24,128]{3,2,1,0:T(8,128)(2,1)S(1)}, bf16[2,8,24,128]{3,2,1,0:T(8,128)(2,1)S(1)}, u32[]{:S(2)}, u32[]{:S(2)}) collective-permute-start(bf16[2,8,24,128]{3,2,1,0:T(8,128)(2,1)S(1)} %get-tuple-element.33), channel_id=1, source_target_pairs={{0,8},{1,9},{2,10},{3,11},{4,12},{5,13},{6,14},{7,15},{8,16},{9,17... | collective-permute-start | bytes 294920 | tf_op jit(solution)/shard_map/ppermute | solution.py:452
  2.4 2.6 %collective-permute-start.1 = (bf16[2,8,8,128]{3,2,1,0:T(8,128)(2,1)S(1)}, bf16[2,8,8,128]{3,2,1,0:T(8,128)(2,1)S(1)}, u32[]{:S(2)}, u32[]{:S(2)}) collective-permute-start(bf16[2,8,8,128]{3,2,1,0:T(8,128)(2,1)S(1)} %get-tuple-element.34), channel_id=1, source_target_pairs={{0,1},{1,2},{2,3},{3,4},{4,5},{5,6},{6,7},{7,0},{8,9},{9,10},{10,1... | collective-permute-start | bytes 98312 | tf_op jit(solution)/shard_map/ppermute | solution.py:452
  4.9 2.4 %collective-permute-start.2 = (bf16[2,8,8,128]{3,2,1,0:T(8,128)(2,1)S(1)}, bf16[2,8,8,128]{3,2,1,0:T(8,128)(2,1)S(1)}, u32[]{:S(2)}, u32[]{:S(2)}) collective-permute-start(bf16[2,8,8,128]{3,2,1,0:T(8,128)(2,1)S(1)} %get-tuple-element.35), channel_id=1, source_target_pairs={{0,9},{1,10},{2,11},{3,12},{4,13},{5,14},{6,15},{7,8},{8,17},{9,18... | collective-permute-start | bytes 98312 | tf_op jit(solution)/shard_map/ppermute | solution.py:452
  7.3 0.9 %bias.1.refs_3_.refs_8_ = f32[2,1024,256]{2,1,0:T(8,128)S(1)} custom-call(f32[31,4,31]{2,1,0:T(4,128)S(1)} %get-tuple-element.36.table_ref), custom_call_target="tpu_custom_call" | custom-call | flops 8000000 | bytes 2000000 | tf_op jit(solution)/shard_map/bias/pallas_call | solution.py:490
  8.3 0.0 collective-permute-done.refs_2_
  8.3 3.2 %first.1 = (bf16[2,8,16,128]{3,2,1,0:T(8,128)(2,1)S(1)}, bf16[2,8,16,128]{3,2,1,0:T(8,128)(2,1)S(1)}, f32[1536,128]{1,0:T(8,128)S(1)}, f32[64,512]{1,0:T(8,128)S(1)}, f32[8,128]{1,0:T(8,128)S(1)}) custom-call(bf16[16,32,128]{2,1,0:T(8,128)(2,1)S(1)} %copy-done, bf16[16,32,128]{2,1,0:T(8,128)(2,1)S(1)} %copy-done.1, ...), custom_call_target="tpu_custom_call" | custom-call | flops 1000000000 | bytes 2000000 | tf_op jit(solution)/shard_map/first/pallas_call | solution.py:534
  11.6 0.0 collective-permute-done.1.refs_3_
  11.6 0.3 collective-permute-done.2.refs_4_
  11.9 3.6 %last.1 = (bf16[2,8,8,128]{3,2,1,0:T(8,128)(2,1)S(1)}, bf16[2,8,8,128]{3,2,1,0:T(8,128)(2,1)S(1)}, bf16[2,8,8,128]{3,2,1,0:T(8,128)(2,1)S(1)}, bf16[2,8,8,128]{3...) custom-call(bf16[16,32,128]{2,1,0:T(8,128)(2,1)S(1)} %copy-done, ...), custom_call_target="tpu_custom_call" | custom-call | flops 1000000000 | bytes 2000000 | tf_op jit(solution)/shard_map/last/pallas_call | solution.py:534
  15.5 0.4 collective-permute-start.3
  15.9 1.1 %collective-permute-done.3.second_ref = bf16[896,128]{1,0:T(8,128)(2,1)S(1)} collective-permute-done((bf16[896,128]{1,0:T(8,128)(2,1)S(1)}, bf16[896,128]{1,0:T(8,128)(2,1)S(1)}, u32[]{:S(2)}, u32[]{:S(2)}) %collective-permute-start.3) | collective-permute-done | bytes 229408 | tf_op jit(solution)/shard_map/ppermute | solution.py:588
  17.1 0.1 pair.1
  17.1 15.1 %all_to_all.10.in_ref = bf16[16,56,128]{2,1,0:T(8,128)(2,1)S(1)} all-to-all(bf16[16,56,128]{2,1,0:T(8,128)(2,1)S(1)} %bitcast.10), channel_id=1, replica_groups={{0,1,2,3,4,5,6,7,16,17,18,19,20,21,22,23},{8,9,10,11,12,13,14,15,24,25,..., dimensions={0} | all-to-all | bytes 458752 | tf_op jit(solution)/shard_map/all_to_all | solution.py:586
  32.2 11.6 %all_to_all.11 = bf16[16,56,128]{2,1,0:T(8,128)(2,1)S(1)} all-to-all(bf16[16,56,128]{2,1,0:T(8,128)(2,1)S(1)} %add.1), channel_id=1, replica_groups={{0,1,2,3,4,5,6,7,16,17,18,19,20,21,22,23},{8,9,10,11,12,13,14,15,24,25,..., dimensions={0} | all-to-all | bytes 458752 | tf_op jit(solution)/shard_map/all_to_all | solution.py:586
  43.8 0.0 collective-permute-start.4
  43.8 1.4 %collective-permute-start.6 = (bf16[2,8,16,128]{3,2,1,0:T(8,128)(2,1)S(1)}, bf16[2,8,16,128]{3,2,1,0:T(8,128)(2,1)S(1)}, u32[]{:S(2)}, u32[]{:S(2)}) collective-permute-start(bf16[2,8,16,128]{3,2,1,0:T(8,128)(2,1)S(1)} %get-tuple-element.43), channel_id=1, source_target_pairs={{0,24},{1,25},{2,26},{3,27},{4,28},{5,29},{6,30},{7,31},{8,0},{9,1... | collective-permute-start | bytes 196616 | tf_op jit(solution)/shard_map/ppermute | solution.py:452
  45.3 0.7 %collective-permute-start.5 = (bf16[2,8,8,128]{3,2,1,0:T(8,128)(2,1)S(1)}, bf16[2,8,8,128]{3,2,1,0:T(8,128)(2,1)S(1)}, u32[]{:S(2)}, u32[]{:S(2)}) collective-permute-start(bf16[2,8,8,128]{3,2,1,0:T(8,128)(2,1)S(1)} %get-tuple-element.42), channel_id=1, source_target_pairs={{0,31},{1,24},{2,25},{3,26},{4,27},{5,28},{6,29},{7,30},{8,7},{9,0... | collective-permute-start | bytes 98312 | tf_op jit(solution)/shard_map/ppermute | solution.py:452
  46.0 1.9 %collective-permute-start.7 = (bf16[2,8,8,128]{3,2,1,0:T(8,128)(2,1)S(1)}, bf16[2,8,8,128]{3,2,1,0:T(8,128)(2,1)S(1)}, u32[]{:S(2)}, u32[]{:S(2)}) collective-permute-start(bf16[2,8,8,128]{3,2,1,0:T(8,128)(2,1)S(1)} %get-tuple-element.44), channel_id=1, source_target_pairs={{0,24},{1,25},{2,26},{3,27},{4,28},{5,29},{6,30},{7,31},{8,0},{9,1... | collective-permute-start | bytes 98312 | tf_op jit(solution)/shard_map/ppermute | solution.py:452
  47.9 1.5 %collective-permute-start.8 = (bf16[2,8,8,128]{3,2,1,0:T(8,128)(2,1)S(1)}, bf16[2,8,8,128]{3,2,1,0:T(8,128)(2,1)S(1)}, u32[]{:S(2)}, u32[]{:S(2)}) collective-permute-start(bf16[2,8,8,128]{3,2,1,0:T(8,128)(2,1)S(1)} %get-tuple-element.45), channel_id=1, source_target_pairs={{0,7},{1,0},{2,1},{3,2},{4,3},{5,4},{6,5},{7,6},{8,15},{9,8},{10,9... | collective-permute-start | bytes 98312 | tf_op jit(solution)/shard_map/ppermute | solution.py:452
  49.4 0.0 collective-permute-done.5.diag_ref
  49.4 0.1 collective-permute-done.7.above_last_ref
  49.5 2.3 %collective-permute-done.8.left_ref = bf16[2,8,8,128]{3,2,1,0:T(8,128)(2,1)S(1)} collective-permute-done((bf16[2,8,8,128]{3,2,1,0:T(8,128)(2,1)S(1)}, bf16[2,8,8,128]{3,2,1,0:T(8,128)(2,1)S(1)}, u32[]{:S(2)}, u32[]{:S(2)}) %collective-permute-start.8) | collective-permute-done | bytes 32800 | tf_op jit(solution)/shard_map/ppermute | solution.py:452
  51.8 0.0 collective-permute-done.6.above_first_ref
  51.8 0.0 collective-permute-done.4.other_ref
  51.8 1.0 %unpack.1 = (bf16[16,32,128]{2,1,0:T(8,128)(2,1)}, bf16[16,32,128]{2,1,0:T(8,128)(2,1)}, f32[1,128]{1,0:T(1,128)}, f32[128,384]{1,0:T(8,128)}, f32[128,128]{1,0:...) custom-call(bf16[896,128]{1,0:T(8,128)(2,1)S(1)} %bitcast.9, ...), custom_call_target="tpu_custom_call" | custom-call | tf_op jit(solution)/shard_map/unpack/pallas_call | solution.py:619
  (11 shorter events, 0.1 us)
Async XLA Ops:
  0.6 7.6 %copy-start.1 = (bf16[16,32,128]{2,1,0:T(8,128)(2,1)S(1)}, bf16[16,32,128]{2,1,0:T(8,128)(2,1)}, u32[]{:S(2)}) copy-start(bf16[16,32,128]{2,1,0:T(8,128)(2,1)} %refs_1_.3) | copy-start | bytes 393220
  0.7 7.6 %copy-start = (bf16[16,32,128]{2,1,0:T(8,128)(2,1)S(1)}, bf16[16,32,128]{2,1,0:T(8,128)(2,1)}, u32[]{:S(2)}) copy-start(bf16[16,32,128]{2,1,0:T(8,128)(2,1)} %refs_0_.3) | copy-start | bytes 393220
  0.7 7.6 %copy-start.3 = (bf16[512,128]{1,0:T(8,128)(2,1)S(1)}, bf16[512,128]{1,0:T(8,128)(2,1)}, u32[]{:S(2)}) copy-start(bf16[512,128]{1,0:T(8,128)(2,1)} %refs_14_.1) | copy-start | bytes 393220
  0.7 7.6 %copy-start.2 = (bf16[128,512]{1,0:T(8,128)(2,1)S(1)}, bf16[128,512]{1,0:T(8,128)(2,1)}, u32[]{:S(2)}) copy-start(bf16[128,512]{1,0:T(8,128)(2,1)} %refs_13_.1) | copy-start | bytes 393220
  0.7 7.6 %copy-start.5 = (bf16[128,128]{1,0:T(8,128)(2,1)S(1)}, bf16[128,128]{1,0:T(8,128)(2,1)}, u32[]{:S(2)}) copy-start(bf16[128,128]{1,0:T(8,128)(2,1)} %refs_11_.1) | copy-start | bytes 98308
  0.7 7.6 %copy-start.4 = (bf16[128,384]{1,0:T(8,128)(2,1)S(1)}, bf16[128,384]{1,0:T(8,128)(2,1)}, u32[]{:S(2)}) copy-start(bf16[128,384]{1,0:T(8,128)(2,1)} %refs_10_.1) | copy-start | bytes 294916
  0.7 7.6 %copy-start.7 = (f32[128]{0:T(128)S(1)}, f32[128]{0:T(128)}, u32[]{:S(2)}) copy-start(f32[128]{0:T(128)} %param.14) | copy-start | bytes 1540
  0.7 7.6 %copy-start.6 = (f32[128]{0:T(128)S(1)}, f32[128]{0:T(128)}, u32[]{:S(2)}) copy-start(f32[128]{0:T(128)} %param.10) | copy-start | bytes 1540
  1.8 6.4 %collective-permute-start = (bf16[2,8,24,128]{3,2,1,0:T(8,128)(2,1)S(1)}, bf16[2,8,24,128]{3,2,1,0:T(8,128)(2,1)S(1)}, u32[]{:S(2)}, u32[]{:S(2)}) collective-permute-start(bf16[2,8,24,128]{3,2,1,0:T(8,128)(2,1)S(1)} %get-tuple-element.33), channel_id=1, source_target_pairs={{0,8},{1,9},{2,10},{3,11},{4,12},{5,13},{6,14},{7,15},{8,16},{9,17... | collective-permute-start | bytes 294920 | tf_op jit(solution)/shard_map/ppermute | solution.py:452
  2.4 9.2 %collective-permute-start.1 = (bf16[2,8,8,128]{3,2,1,0:T(8,128)(2,1)S(1)}, bf16[2,8,8,128]{3,2,1,0:T(8,128)(2,1)S(1)}, u32[]{:S(2)}, u32[]{:S(2)}) collective-permute-start(bf16[2,8,8,128]{3,2,1,0:T(8,128)(2,1)S(1)} %get-tuple-element.34), channel_id=1, source_target_pairs={{0,1},{1,2},{2,3},{3,4},{4,5},{5,6},{6,7},{7,0},{8,9},{9,10},{10,1... | collective-permute-start | bytes 98312 | tf_op jit(solution)/shard_map/ppermute | solution.py:452
  4.9 6.9 %collective-permute-start.2 = (bf16[2,8,8,128]{3,2,1,0:T(8,128)(2,1)S(1)}, bf16[2,8,8,128]{3,2,1,0:T(8,128)(2,1)S(1)}, u32[]{:S(2)}, u32[]{:S(2)}) collective-permute-start(bf16[2,8,8,128]{3,2,1,0:T(8,128)(2,1)S(1)} %get-tuple-element.35), channel_id=1, source_target_pairs={{0,9},{1,10},{2,11},{3,12},{4,13},{5,14},{6,15},{7,8},{8,17},{9,18... | collective-permute-start | bytes 98312 | tf_op jit(solution)/shard_map/ppermute | solution.py:452
  15.5 1.6 %collective-permute-start.3 = (bf16[896,128]{1,0:T(8,128)(2,1)S(1)}, bf16[896,128]{1,0:T(8,128)(2,1)S(1)}, u32[]{:S(2)}, u32[]{:S(2)}) collective-permute-start(bf16[896,128]{1,0:T(8,128)(2,1)S(1)} %get-tuple-element.41), channel_id=1, source_target_pairs={{0,8},{1,9},{2,10},{3,11},{4,12},{5,13},{6,14},{7,15},{8,0},{9,1},... | collective-permute-start | bytes 688136 | tf_op jit(solution)/shard_map/ppermute | solution.py:588
  43.8 8.0 %collective-permute-start.4 = (bf16[896,128]{1,0:T(8,128)(2,1)S(1)}, bf16[896,128]{1,0:T(8,128)(2,1)S(1)}, u32[]{:S(2)}, u32[]{:S(2)}) collective-permute-start(bf16[896,128]{1,0:T(8,128)(2,1)S(1)} %bitcast.8), channel_id=1, source_target_pairs={{0,8},{1,9},{2,10},{3,11},{4,12},{5,13},{6,14},{7,15},{8,0},{9,1},... | collective-permute-start | bytes 688136 | tf_op jit(solution)/shard_map/ppermute | solution.py:606
  43.8 8.0 %collective-permute-start.6 = (bf16[2,8,16,128]{3,2,1,0:T(8,128)(2,1)S(1)}, bf16[2,8,16,128]{3,2,1,0:T(8,128)(2,1)S(1)}, u32[]{:S(2)}, u32[]{:S(2)}) collective-permute-start(bf16[2,8,16,128]{3,2,1,0:T(8,128)(2,1)S(1)} %get-tuple-element.43), channel_id=1, source_target_pairs={{0,24},{1,25},{2,26},{3,27},{4,28},{5,29},{6,30},{7,31},{8,0},{9,1... | collective-permute-start | bytes 196616 | tf_op jit(solution)/shard_map/ppermute | solution.py:452
  45.3 4.1 %collective-permute-start.5 = (bf16[2,8,8,128]{3,2,1,0:T(8,128)(2,1)S(1)}, bf16[2,8,8,128]{3,2,1,0:T(8,128)(2,1)S(1)}, u32[]{:S(2)}, u32[]{:S(2)}) collective-permute-start(bf16[2,8,8,128]{3,2,1,0:T(8,128)(2,1)S(1)} %get-tuple-element.42), channel_id=1, source_target_pairs={{0,31},{1,24},{2,25},{3,26},{4,27},{5,28},{6,29},{7,30},{8,7},{9,0... | collective-permute-start | bytes 98312 | tf_op jit(solution)/shard_map/ppermute | solution.py:452
  46.0 3.5 %collective-permute-start.7 = (bf16[2,8,8,128]{3,2,1,0:T(8,128)(2,1)S(1)}, bf16[2,8,8,128]{3,2,1,0:T(8,128)(2,1)S(1)}, u32[]{:S(2)}, u32[]{:S(2)}) collective-permute-start(bf16[2,8,8,128]{3,2,1,0:T(8,128)(2,1)S(1)} %get-tuple-element.44), channel_id=1, source_target_pairs={{0,24},{1,25},{2,26},{3,27},{4,28},{5,29},{6,30},{7,31},{8,0},{9,1... | collective-permute-start | bytes 98312 | tf_op jit(solution)/shard_map/ppermute | solution.py:452
  47.9 3.9 %collective-permute-start.8 = (bf16[2,8,8,128]{3,2,1,0:T(8,128)(2,1)S(1)}, bf16[2,8,8,128]{3,2,1,0:T(8,128)(2,1)S(1)}, u32[]{:S(2)}, u32[]{:S(2)}) collective-permute-start(bf16[2,8,8,128]{3,2,1,0:T(8,128)(2,1)S(1)} %get-tuple-element.45), channel_id=1, source_target_pairs={{0,7},{1,0},{2,1},{3,2},{4,3},{5,4},{6,5},{7,6},{8,15},{9,8},{10,9... | collective-permute-start | bytes 98312 | tf_op jit(solution)/shard_map/ppermute | solution.py:452
where the time goes:
time: 53.1 us; the launch traced here: 52.8 us
  blocking collectives  26.7 us (50%)
  starting transfers between devices  11.5 us (22%)
  Pallas kernels  10 us (19%)
  waiting for transfers between devices  3.85 us (7%)
  between operations  0.83 us (2%)
    all_to_all x2, blocking collectives, exchanged(): lax.all_to_all(value, AXES, 0, 0, tiled=True, axis_index_groups=same_core)  26.7 us
    ppermute x7, starting transfers between devices, passed_along(): return lax.ppermute(value, AXES, neighbour_pairs(row_step, col_step))  11 us
    pallas_call x2, Pallas kernels, block(): pl.pallas_call(functools.partial(block_kernel, heads, first, count, last)...  6.88 us
    ppermute x7, waiting for transfers between devices, passed_along(): return lax.ppermute(value, AXES, neighbour_pairs(row_step, col_step))  2.71 us
    ppermute x1, waiting for transfers between devices, shards(): received = lax.ppermute(sent, AXES, pairs)  1.13 us
    pallas_call x1, Pallas kernels, shards(): pl.pallas_call(cut_kernel, out_shape=(array((2, SHIFT, keep, width)), arr...  1.08 us
  transfers between devices with their start and end apart: 9, of which 4 were waited for; matrix products, arithmetic and copies ran while one was open for 0% of the time, Pallas kernels for 8%

commit v1 on v0

--- a/solution.py
+++ b/solution.py
@@ -134,92 +134,103 @@
         each.wait()
 
 
-def block_kernel(heads, first, count, last, *refs):
-    token_ref, cot_ref, below_ref = refs[:3]
-    refs = refs[3:]
-    if last:
-        right_ref, diag_ref, sums_in, strip_in, gains_in = refs[:5]
-        refs = refs[5:]
-    bias_ref, gain1_ref, qkv_ref, proj_ref, gain2_ref, fc1_ref, fc2_ref = refs[:7]
-    own_out, below_out = refs[7:9]
-    refs = refs[9:]
-    if last:
-        right_out, diag_out, keep_out, send_out, grads_ref = refs[:5]
-        refs = refs[5:]
+STATE = ("x", "n", "unit", "scale", "q", "k", "v", "p", "att", "out", "inverse")
+
+
+def assemble(tile_ref, piece_refs, index, window, windows):
+    tile = tile_ref[...].astype(F32)
+    above = piece_refs[0][index].astype(F32)
+    cols = slice(WIN * window + SHIFT, WIN * window + SHIFT + WIN)
+    if window == windows - 1:
+        left = piece_refs[1][index].astype(F32)
+        diag = piece_refs[2][index].astype(F32)
+        top = jnp.concatenate([diag, above[:, :SHIFT]], 1)
+        low = jnp.concatenate([left, tile[:SHIFT, :SHIFT]], 1)
     else:
-        sums_out, strip_out, gains_out = refs[:3]
-        refs = refs[3:]
-    x_ref, c_ref, n_ref, unit_ref, scale_ref, q_ref, k_ref, v_ref = refs[:8]
-    p_ref, att_ref, out_f32_ref, inverse_ref, dh_ref, dqkv_ref, ds_ref, dsn_ref = refs[8:16]
-    inner_ref, before_ref, out_ref = refs[16:]
+        top = above[:, cols]
+        low = tile[:SHIFT, cols]
+    return jnp.concatenate([top, low], 0).reshape(WIN * WIN, tile.shape[2])
+
+
+def of_head(values, head, head_size):
+    lane_head = iota((1, values.shape[1]), 1) // head_size
+    return jnp.where(lane_head == head, values, 0.0).astype(BF16)
+
+
+def attend(heads, window, bias_ref, gain1_ref, qkv_ref, state):
+    tokens, width = state["x"].shape
+    head_size = width // heads
+    unit, scale = norm(state["x"][...])
+    state["unit"][...] = unit
+    state["scale"][...] = scale
+    normed = (unit * gain1_ref[...]).astype(BF16)
+    state["n"][...] = normed
+    projected = dot(normed, qkv_ref[...], 1, 0)
+    state["q"][...] = projected[:, :width]
+    state["k"][...] = projected[:, width : 2 * width].astype(BF16)
+    state["v"][...] = projected[:, 2 * width :].astype(BF16)
+    query = state["q"][...]
+    keys = state["k"][...]
+    value = state["v"][...].astype(F32)
+    sources = []
+    for head in range(heads):
+        rows = slice(head * tokens, (head + 1) * tokens)
+        scores = dot(of_head(query, head, head_size), keys, 1, 1) * (head_size ** (-0.5) * LOG2_E)
+        scores = scores + bias_ref[window, rows, :]
+        weights = jnp.exp2(scores - jnp.max(scores, axis=-1, keepdims=True))
+        state["p"][:, rows] = weights.astype(BF16)
+        ones = jnp.broadcast_to(of_head(jnp.ones((1, width), F32), head, head_size), (tokens, width))
+        sources.append(jnp.concatenate([of_head(value, head, head_size), ones], 1))
+    both = dot(state["p"][...], jnp.concatenate(sources, 0), 1, 0)
+    inverse = 1.0 / both[:, width:]
+    attended = both[:, :width] * inverse
+    state["inverse"][...] = inverse
+    state["out"][...] = attended
+    state["att"][...] = attended.astype(BF16)
+
+
+def early_kernel(heads, windows, token_ref, below_ref, bias_ref, gain1_ref, qkv_ref, *refs):
+    for window in range(windows - 1):
+        state = dict(zip(STATE, refs[window * len(STATE) : (window + 1) * len(STATE)]))
+        state["x"][...] = assemble(token_ref, (below_ref,), 0, window, windows)
+        attend(heads, window, bias_ref, gain1_ref, qkv_ref, state)
+
+
+def block_kernel(heads, windows, *refs):
+    token_ref, cot_ref, below_ref, right_ref, diag_ref = refs[:5]
+    bias_ref, gain1_ref, qkv_ref, proj_ref, gain2_ref, fc1_ref, fc2_ref = refs[5:12]
+    refs = refs[12:]
+    states = []
+    for _ in range(windows - 1):
+        states.append(dict(zip(STATE, refs)))
+        refs = refs[len(STATE) :]
+    own_out, below_out, right_out, diag_out, keep_out, send_out = refs[:6]
+    grads_ref, c_ref, dqkv_ref, ds_ref, dsn_ref, inner_ref, before_ref, out_ref = refs[6:14]
+    states.append(dict(zip(STATE, refs[14:])))
+    count = windows
 
     tokens = WIN * WIN
     width = token_ref.shape[2]
     head_size = width // heads
     hidden_units = fc1_ref.shape[1]
+    score_scale = head_size ** (-0.5)
+    lane_head = iota((1, width), 1) // head_size
+    pieces = (below_ref, right_ref, diag_ref)
 
     def put(row, value):
-        rows = slice(row, row + value.shape[0])
-        if last:
-            grads_ref[rows, :] = (sums_in[rows, :] + value).astype(BF16)
-        else:
-            sums_out[rows, :] = value
-
-    def assemble(tile_ref, index, target):
-        tile = tile_ref[...].astype(F32)
-        above = below_ref[index].astype(F32)
-        for window in range(count):
-            cols = slice(WIN * (first + window) + SHIFT, WIN * (first + window) + SHIFT + WIN)
-            if last and window == count - 1:
-                left = right_ref[index].astype(F32)
-                diag = diag_ref[index].astype(F32)
-                top = jnp.concatenate([diag, above[:, :SHIFT]], 1)
-                low = jnp.concatenate([left, tile[:SHIFT, :SHIFT]], 1)
-            else:
-                top = above[:, cols]
-                low = tile[:SHIFT, cols]
-            both = jnp.concatenate([top, low], 0).reshape(tokens, width)
-            target[window * tokens : (window + 1) * tokens, :] = both.astype(target.dtype)
-
-    assemble(token_ref, 0, x_ref)
-    assemble(cot_ref, 1, c_ref)
-
-    unit1, scale1 = norm(x_ref[...])
-    unit_ref[...] = unit1
-    scale_ref[...] = scale1
-    normed = (unit1 * gain1_ref[...]).astype(BF16)
-    n_ref[...] = normed
-    projected = dot(normed, qkv_ref[...], 1, 0)
-    q_ref[...] = projected[:, :width]
-    k_ref[...] = projected[:, width : 2 * width].astype(BF16)
-    v_ref[...] = projected[:, 2 * width :].astype(BF16)
-    lane_head = iota((1, width), 1) // head_size
-    score_scale = head_size ** (-0.5)
-
-    def of_head(values, head):
-        return jnp.where(lane_head == head, values, 0.0).astype(BF16)
-
-    for window in range(count):
-        span = slice(window * tokens, (window + 1) * tokens)
-        query = q_ref[span, :]
-        keys = k_ref[span, :]
-        value = v_ref[span, :].astype(F32)
-        sources = []
-        for head in range(heads):
-            scores = dot(of_head(query, head), keys, 1, 1) * (score_scale * LOG2_E)
-            scores = scores + bias_ref[first + window, head * tokens : (head + 1) * tokens, :]
-            weights = jnp.exp2(scores - jnp.max(scores, axis=-1, keepdims=True))
-            p_ref[window, :, head * tokens : (head + 1) * tokens] = weights.astype(BF16)
-            ones = jnp.broadcast_to(of_head(jnp.ones((1, width), F32), head), (tokens, width))
-            sources.append(jnp.concatenate([of_head(value, head), ones], 1))
-        both = dot(p_ref[window], jnp.concatenate(sources, 0), 1, 0)
-        inverse = 1.0 / both[:, width:]
-        attended = both[:, :width] * inverse
-        inverse_ref[span, :] = inverse
-        out_f32_ref[span, :] = attended
-        att_ref[span, :] = attended.astype(BF16)
-
-    hidden = x_ref[...] + dot(att_ref[...], proj_ref[...], 1, 0).astype(BF16).astype(F32)
+        grads_ref[row : row + value.shape[0], :] = value.astype(BF16)
+
+    def stacked(name):
+        return jnp.concatenate([state[name][...] for state in states], 0)
+
+    states[-1]["x"][...] = assemble(token_ref, pieces, 0, windows - 1, windows)
+    for window in range(windows):
+        piece = assemble(cot_ref, pieces, 1, window, windows)
+        c_ref[window * tokens : (window + 1) * tokens, :] = piece.astype(BF16)
+    attend(heads, windows - 1, bias_ref, gain1_ref, qkv_ref, states[-1])
+
+    attended = stacked("att")
+    hidden = stacked("x") + dot(attended, proj_ref[...], 1, 0).astype(BF16).astype(F32)
     unit2, scale2 = norm(hidden)
     normed2 = (unit2 * gain2_ref[...]).astype(BF16)
     cot = c_ref[...]
@@ -244,20 +255,20 @@
     put(hidden_units, dot(inner, cot, 0, 0))
     grad_gain2 = jnp.sum(back * unit2, axis=0, keepdims=True)
     grad_hidden = cot.astype(F32) + norm_back(back * gain2_ref[...], unit2, scale2)
-    dh_ref[...] = grad_hidden
 
     grad_attended = grad_hidden.astype(BF16)
-    put(2 * hidden_units + 3 * width, dot(att_ref[...], grad_attended, 0, 0))
+    put(2 * hidden_units + 3 * width, dot(attended, grad_attended, 0, 0))
     grad_heads = dot(grad_attended, proj_ref[...], 1, 1).astype(BF16).astype(F32)
 
     minus = jnp.full((tokens, width), -1.0, BF16)
     for window in range(count):
         span = slice(window * tokens, (window + 1) * tokens)
-        query = q_ref[span, :]
-        keys = k_ref[span, :].astype(F32)
-        value = jnp.concatenate([v_ref[span, :], minus], 1)
-        scaled = (grad_heads[span, :] * inverse_ref[span, :]).astype(BF16).astype(F32)
-        inside = scaled * out_f32_ref[span, :]
+        state = states[window]
+        query = state["q"][...]
+        keys = state["k"][...].astype(F32)
+        value = jnp.concatenate([state["v"][...], minus], 1)
+        scaled = (grad_heads[span, :] * state["inverse"][...]).astype(BF16).astype(F32)
+        inside = scaled * state["out"][...]
         inside_high = inside.astype(BF16).astype(F32)
         inside_low = pltpu.roll(inside - inside_high, head_size, 1)
         query_t = query.T.astype(BF16)
@@ -271,8 +282,8 @@
                 inside_high,
                 jnp.where(lane_head == (head + 1) % heads, inside_low, 0.0),
             ).astype(BF16)
-            grad_weights = dot(jnp.concatenate([of_head(scaled, head), extra], 1), value, 1, 1)
-            weights = p_ref[window, :, rows]
+            grad_weights = dot(jnp.concatenate([of_head(scaled, head, head_size), extra], 1), value, 1, 1)
+            weights = state["p"][:, rows]
             grad_scores = grad_weights * weights.astype(F32)
             if window == 0:
                 ds_ref[rows, :] = grad_scores
@@ -280,7 +291,7 @@
                 ds_ref[rows, :] += grad_scores
             narrow = grad_scores.astype(BF16)
             dsn_ref[:, rows] = narrow
-            sources.append(of_head(keys, head))
+            sources.append(of_head(keys, head, head_size))
             grad_k.append(dot(query_t[part, :], narrow, 1, 0))
             grad_v.append(dot(scaled_t[part, :], weights, 1, 0))
         grad_q = dot(dsn_ref[...], jnp.concatenate(sources, 0), 1, 0)
@@ -290,19 +301,19 @@
         dqkv_ref[span, 2 * width :] = jnp.concatenate(grad_v, 0).T.astype(BF16)
 
     grad_projected = dqkv_ref[...]
-    grad_qkv = dot(n_ref[...], grad_projected, 0, 0)
+    grad_qkv = dot(stacked("n"), grad_projected, 0, 0)
     for part in range(3):
         put(2 * hidden_units + part * width, grad_qkv[:, part * width : (part + 1) * width])
     grad_normed = dot(grad_projected, qkv_ref[...], 1, 1).astype(BF16).astype(F32)
-    unit1 = unit_ref[...]
+    unit1 = stacked("unit")
     grad_gain1 = jnp.sum(grad_normed * unit1, axis=0, keepdims=True)
-    grad_x = dh_ref[...] + norm_back(grad_normed * gain1_ref[...], unit1, scale_ref[...])
+    grad_x = grad_hidden + norm_back(grad_normed * gain1_ref[...], unit1, stacked("scale"))
     gains = jnp.concatenate([grad_gain1, grad_gain2, jnp.zeros((6, width), F32)], 0)
 
     lanes = 2 * tokens
     rows = heads * WIN
     blank = jnp.zeros((WIN, LANES), F32)
-    strip = strip_in[...] if last else jnp.zeros((rows, lanes), F32)
+    strip = jnp.zeros((rows, lanes), F32)
     for fine in range(8):
         near, far = WIN - 1 - fine, WIN - 9 - fine
         blocks = []
@@ -315,25 +326,21 @@
         block = jnp.concatenate(blocks, 0)
         strip = strip + (pltpu.roll(block, WIN * fine, 1) if fine else block)
 
-    if last:
-        finish_table(heads, strip, grads_ref, 2 * hidden_units + 4 * width)
-        row = 2 * hidden_units + 4 * width + heads * 2 * WIN
-        blank = jnp.zeros((grads_ref.shape[0] - row - 8, width), F32)
-        grads_ref[row:, :] = jnp.concatenate([gains_in[...] + gains, blank], 0).astype(BF16)
-        half = keep_out.shape[0]
-        core = lax.axis_index("group") % 2
-        keep_out[...] = grads_ref[pl.ds(pl.multiple_of(core * half, 16), half), :]
-        send_out[...] = grads_ref[pl.ds(pl.multiple_of((1 - core) * half, 16), half), :]
-    else:
-        strip_out[...] = strip
-        gains_out[...] = gains
+    finish_table(heads, strip, grads_ref, 2 * hidden_units + 4 * width)
+    row = 2 * hidden_units + 4 * width + heads * 2 * WIN
+    blank = jnp.zeros((grads_ref.shape[0] - row - 8, width), F32)
+    grads_ref[row:, :] = jnp.concatenate([gains, blank], 0).astype(BF16)
+    half = keep_out.shape[0]
+    core = lax.axis_index("group") % 2
+    keep_out[...] = grads_ref[pl.ds(pl.multiple_of(core * half, 16), half), :]
+    send_out[...] = grads_ref[pl.ds(pl.multiple_of((1 - core) * half, 16), half), :]
 
     for index, values in enumerate((out_ref[...], grad_x)):
         for window in range(count):
             start = WIN * window
             block = values[window * tokens : (window + 1) * tokens, :].reshape(WIN, WIN, width)
             top, low = block[:SHIFT], block[SHIFT:]
-            if last and window == count - 1:
+            if window == count - 1:
                 own_out[index, :, start:, :] = low[:, SHIFT:].astype(BF16)
                 below_out[index, :, start:, :] = top[:, SHIFT:].astype(BF16)
                 right_out[index] = low[:, :SHIFT].astype(BF16)
@@ -387,11 +394,9 @@
     mine_ref,
     other_ref,
     diag_ref,
-    above_first_ref,
-    above_last_ref,
+    above_ref,
     left_ref,
-    own_first_ref,
-    own_last_ref,
+    own_ref,
     out_ref,
     grad_ref,
     gain1_ref,
@@ -405,13 +410,13 @@
 ):
     width, hidden_units = fc1_ref.shape
     half = mine_ref.shape[0]
-    early = own_first_ref.shape[2]
+    early = own_ref.shape[2] - SHIFT
+    cuts = ((slice(0, SHIFT), slice(early, None)), (slice(SHIFT, SHIFT + early), slice(0, early)))
     for index, target in enumerate((out_ref, grad_ref)):
-        target[:SHIFT, :SHIFT, :] = own_last_ref[index]
-        target[:SHIFT, SHIFT : SHIFT + early, :] = own_first_ref[index]
+        for cols, source in cuts:
+            target[:SHIFT, cols, :] = own_ref[index, :, source, :]
+            target[SHIFT:, cols, :] = above_ref[index, :, source, :]
         target[:SHIFT, SHIFT + early :, :] = left_ref[index]
-        target[SHIFT:, :SHIFT, :] = above_last_ref[index]
-        target[SHIFT:, SHIFT : SHIFT + early, :] = above_first_ref[index]
         target[SHIFT:, SHIFT + early :, :] = diag_ref[index]
     core = lax.axis_index("group") % 2
     summed_ref[pl.ds(pl.multiple_of(core * half, 16), half), :] = mine_ref[...]
@@ -503,24 +508,39 @@
     chunk = (used + devices * 8 - 1) // (devices * 8) * 8
     half = chunk * members
     weights = (gain1.reshape(1, width), w_qkv, w_proj, gain2.reshape(1, width), w_fc1, w_fc2)
-    sum_rows = 2 * hidden_units + 4 * width
-
-    def block(first, count, last, inputs, outputs):
-        total = count * token_count
-        scratch = [
-            pltpu.VMEM((total, width), F32),
+    total = windows * token_count
+    state_types = dict.fromkeys(STATE, ((token_count, width), F32))
+    state_types["scale"] = ((token_count, 1), F32)
+    for name in ("n", "k", "v", "att"):
+        state_types[name] = ((token_count, width), BF16)
+    state_types["p"] = ((token_count, heads * token_count), BF16)
+    states = pl.pallas_call(
+        functools.partial(early_kernel, heads, windows),
+        out_shape=[array(*state_types[name]) for name in STATE] * (windows - 1),
+        in_specs=[vmem] * 5,
+        out_specs=[vmem] * (len(STATE) * (windows - 1)),
+        name="early",
+        compiler_params=PARAMS,
+        cost_estimate=pl.CostEstimate(
+            flops=500_000_000, bytes_accessed=2_000_000, transcendentals=500_000
+        ),
+    )(tokens, below, bias, weights[0], w_qkv)
+    inputs = (tokens, cotangent, below, right, diag, bias) + weights + tuple(states)
+    own_out, below_out, right_out, diag_out, kept, sent = pl.pallas_call(
+        functools.partial(block_kernel, heads, windows),
+        out_shape=(
+            array((2, SHIFT, keep, width)),
+            array((2, SHIFT, keep, width)),
+            array((2, SHIFT, SHIFT, width)),
+            array((2, SHIFT, SHIFT, width)),
+            array((half, width)),
+            array((half, width)),
+        ),
+        in_specs=[vmem] * len(inputs),
+        out_specs=(vmem,) * 6,
+        scratch_shapes=[
+            pltpu.VMEM((2 * half, width), BF16),
             pltpu.VMEM((total, width), BF16),
-            pltpu.VMEM((total, width), BF16),
-            pltpu.VMEM((total, width), F32),
-            pltpu.VMEM((total, 1), F32),
-            pltpu.VMEM((total, width), F32),
-            pltpu.VMEM((total, width), BF16),
-            pltpu.VMEM((total, width), BF16),
-            pltpu.VMEM((count, token_count, heads * token_count), BF16),
-            pltpu.VMEM((total, width), BF16),
-            pltpu.VMEM((total, width), F32),
-            pltpu.VMEM((total, width), F32),
-            pltpu.VMEM((total, width), F32),
             pltpu.VMEM((total, 3 * width), BF16),
             pltpu.VMEM((heads * token_count, token_count), F32),
             pltpu.VMEM((token_count, heads * token_count), BF16),
@@ -528,54 +548,16 @@
             pltpu.VMEM((total, hidden_units), BF16),
             pltpu.VMEM((total, width), F32),
         ]
-        if last:
-            scratch = [pltpu.VMEM((2 * half, width), BF16)] + scratch
-        inputs = inputs + (bias,) + weights
-        return pl.pallas_call(
-            functools.partial(block_kernel, heads, first, count, last),
-            out_shape=outputs,
-            in_specs=[vmem] * len(inputs),
-            out_specs=(vmem,) * len(outputs),
-            scratch_shapes=scratch,
-            name="last" if last else "first",
-            compiler_params=PARAMS,
-            cost_estimate=pl.CostEstimate(
-                flops=1_000_000_000 * count, bytes_accessed=2_000_000, transcendentals=1_000_000
-            ),
-        )(*inputs)
-
-    early = WIN * (windows - 1)
-    own_first, below_first, sums, strip, gains = block(
-        0,
-        windows - 1,
-        False,
-        (tokens, cotangent, below),
-        (
-            array((2, SHIFT, early, width)),
-            array((2, SHIFT, early, width)),
-            array((sum_rows, width), F32),
-            array((heads * WIN, 2 * token_count), F32),
-            array((8, width), F32),
+        + [pltpu.VMEM(*state_types[name]) for name in STATE],
+        name="block",
+        compiler_params=PARAMS,
+        cost_estimate=pl.CostEstimate(
+            flops=1_500_000_000, bytes_accessed=2_000_000, transcendentals=1_000_000
         ),
-    )
-    back_first = passed_along(below_first, -1, 0)
-    own_last, below_last, right_last, diag_last, kept, sent = block(
-        windows - 1,
-        1,
-        True,
-        (tokens, cotangent, below, right, diag, sums, strip, gains),
-        (
-            array((2, SHIFT, SHIFT, width)),
-            array((2, SHIFT, SHIFT, width)),
-            array((2, SHIFT, SHIFT, width)),
-            array((2, SHIFT, SHIFT, width)),
-            array((half, width)),
-            array((half, width)),
-        ),
-    )
-    back_right = passed_along(right_last, 0, -1)
-    back_diag = passed_along(diag_last, -1, -1)
-    back_below = passed_along(below_last, -1, 0)
+    )(*inputs)
+    back_right = passed_along(right_out, 0, -1)
+    back_diag = passed_along(diag_out, -1, -1)
+    back_below = passed_along(below_out, -1, 0)
 
     pairs = [(index, index + tiles if index // tiles % 2 == 0 else index - tiles) for index in range(devices)]
     same_core = [
@@ -629,12 +611,12 @@
             jax.ShapeDtypeStruct(w_fc1.shape, F32),
             jax.ShapeDtypeStruct(w_fc2.shape, F32),
         ),
-        in_specs=[vmem] * 8,
+        in_specs=[vmem] * 6,
         out_specs=(vmem,) * 9,
         scratch_shapes=[pltpu.VMEM((2 * half, width), BF16)],
         name="unpack",
         compiler_params=PARAMS,
-    )(mine, other, back_diag, back_first, back_below, back_right, own_first, own_last)
+    )(mine, other, back_diag, back_below, back_right, own_out)
 
     return (
         block_output,

time: 53.1 us -> 50.9 us (0.959)
  waiting for transfers between devices: 3.85 us -> 6.29 us
  starting transfers between devices: 11.5 us -> 9.73 us
  blocking collectives: 26.7 us -> 25.1 us
  Pallas kernels: 10 us -> 8.77 us
    ppermute x7 -> x6, waiting for transfers between devices: 2.71 us -> 5.16 us  [passed_along(): return lax.ppermute(value, AXES, neighbour_pairs(row_step, col_step))]
    ppermute x7 -> x6, starting transfers between devices: 11 us -> 9.3 us  [passed_along(): return lax.ppermute(value, AXES, neighbour_pairs(row_step, col_step))]
    all_to_all x2, blocking collectives: 26.7 us -> 25.1 us  [exchanged(): lax.all_to_all(value, AXES, 0, 0, tiled=True, axis_index_groups=same_core)]
    pallas_call x2, Pallas kernels: 6.88 us -> 5.67 us  [the longest x1 4.67 us: shards(): pl.pallas_call(functools.partial(block_kernel, heads, windows), out_shape...]
  transfers between devices with their start and end apart: 9 -> 8, of which waited for: 4 -> 5; matrix products, arithmetic and copies ran while one was open for 0% -> 0% of each run, Pallas kernels for 8% -> 4%
where the time goes in v1:
time: 50.9 us; the launch traced here: 50.6 us
  blocking collectives  25.1 us (49%)
  starting transfers between devices  9.73 us (19%)
  Pallas kernels  8.77 us (17%)
  waiting for transfers between devices  6.29 us (12%)
  between operations  0.77 us (2%)
    all_to_all x2, blocking collectives, exchanged(): lax.all_to_all(value, AXES, 0, 0, tiled=True, axis_index_groups=same_core)  25.1 us
    ppermute x6, starting transfers between devices, passed_along(): return lax.ppermute(value, AXES, neighbour_pairs(row_step, col_step))  9.3 us
    ppermute x6, waiting for transfers between devices, passed_along(): return lax.ppermute(value, AXES, neighbour_pairs(row_step, col_step))  5.16 us
    pallas_call x1, Pallas kernels, shards(): pl.pallas_call(functools.partial(block_kernel, heads, windows), out_shape...  4.67 us
    ppermute x1, waiting for transfers between devices, shards(): received = lax.ppermute(sent, AXES, pairs)  1.13 us
    pallas_call x1, Pallas kernels, shards(): pl.pallas_call(cut_kernel, out_shape=(array((2, SHIFT, keep, width)), arr...  1.04 us
  transfers between devices with their start and end apart: 8, of which 5 were waited for; matrix products, arithmetic and copies ran while one was open for 0% of the time, Pallas kernels for 4%

profile of v1, /device:TPU:0, one launch (start us, length us, event | category | flops | bytes accessed | tf_op | source)
XLA Modules:
  0.0 50.6 jit_solution(15588718784176333106)
XLA Ops:
  0.6 0.0 copy-start
  0.7 0.0 copy-start.2
  0.7 0.0 copy-start.3
  0.7 1.0 %cut.1 = (bf16[2,8,24,128]{3,2,1,0:T(8,128)(2,1)S(1)}, bf16[2,8,8,128]{3,2,1,0:T(8,128)(2,1)S(1)}, bf16[2,8,8,128]{3,2,1,0:T(8,128)(2,1)S(1)}, f32[31,4,31]{2,1,0:T(4,128)S(1)}) custom-call(bf16[16,32,128]{2,1,0:T(8,128)(2,1)} %refs_0_.1, bf16[16,32,128]{2,1,0:T(8,128)(2,1)} %refs_1_.1, f32[31,4,31]{2,1,0:T(4,128)} %bitcast.14), custom_call_target="tpu_custom_call" | custom-call | tf_op jit(solution)/shard_map/cut/pallas_call | solution.py:477
  1.7 0.5 %collective-permute-start = (bf16[2,8,24,128]{3,2,1,0:T(8,128)(2,1)S(1)}, bf16[2,8,24,128]{3,2,1,0:T(8,128)(2,1)S(1)}, u32[]{:S(2)}, u32[]{:S(2)}) collective-permute-start(bf16[2,8,24,128]{3,2,1,0:T(8,128)(2,1)S(1)} %get-tuple-element.39), channel_id=1, source_target_pairs={{0,8},{1,9},{2,10},{3,11},{4,12},{5,13},{6,14},{7,15},{8,16},{9,17... | collective-permute-start | bytes 294920 | tf_op jit(solution)/shard_map/ppermute | solution.py:457
  2.3 2.6 %collective-permute-start.1 = (bf16[2,8,8,128]{3,2,1,0:T(8,128)(2,1)S(1)}, bf16[2,8,8,128]{3,2,1,0:T(8,128)(2,1)S(1)}, u32[]{:S(2)}, u32[]{:S(2)}) collective-permute-start(bf16[2,8,8,128]{3,2,1,0:T(8,128)(2,1)S(1)} %get-tuple-element.40), channel_id=1, source_target_pairs={{0,1},{1,2},{2,3},{3,4},{4,5},{5,6},{6,7},{7,0},{8,9},{9,10},{10,1... | collective-permute-start | bytes 98312 | tf_op jit(solution)/shard_map/ppermute | solution.py:457
  4.8 2.4 %collective-permute-start.2 = (bf16[2,8,8,128]{3,2,1,0:T(8,128)(2,1)S(1)}, bf16[2,8,8,128]{3,2,1,0:T(8,128)(2,1)S(1)}, u32[]{:S(2)}, u32[]{:S(2)}) collective-permute-start(bf16[2,8,8,128]{3,2,1,0:T(8,128)(2,1)S(1)} %get-tuple-element.41), channel_id=1, source_target_pairs={{0,9},{1,10},{2,11},{3,12},{4,13},{5,14},{6,15},{7,8},{8,17},{9,18... | collective-permute-start | bytes 98312 | tf_op jit(solution)/shard_map/ppermute | solution.py:457
  7.2 0.0 copy-start.7
  7.2 0.9 %bias.1.bias_ref.refs_5_ = f32[2,1024,256]{2,1,0:T(8,128)S(1)} custom-call(f32[31,4,31]{2,1,0:T(4,128)S(1)} %get-tuple-element.42.table_ref), custom_call_target="tpu_custom_call" | custom-call | flops 8000000 | bytes 2000000 | tf_op jit(solution)/shard_map/bias/pallas_call | solution.py:495
  8.2 0.0 collective-permute-done.below_ref.refs_2_
  8.2 0.0 copy-done
  8.2 0.0 copy-done.2
  8.2 1.0 %early.1 = (f32[256,128]{1,0:T(8,128)S(1)}, bf16[256,128]{1,0:T(8,128)(2,1)S(1)}, f32[256,128]{1,0:T(8,128)S(1)}, f32[256,1]{1,0:T(8,128)S(1)}, f32[256,128]{1,0...) custom-call(bf16[16,32,128]{2,1,0:T(8,128)(2,1)S(1)} %copy-done, ...), custom_call_target="tpu_custom_call" | custom-call | flops 500000000 | bytes 2000000 | tf_op jit(solution)/shard_map/early/pallas_call | solution.py:517
  9.2 0.5 %collective-permute-done.1.refs_3_ = bf16[2,8,8,128]{3,2,1,0:T(8,128)(2,1)S(1)} collective-permute-done((bf16[2,8,8,128]{3,2,1,0:T(8,128)(2,1)S(1)}, bf16[2,8,8,128]{3,2,1,0:T(8,128)(2,1)S(1)}, u32[]{:S(2)}, u32[]{:S(2)}) %collective-permute-start.1) | collective-permute-done | bytes 32800 | tf_op jit(solution)/shard_map/ppermute | solution.py:457
  9.8 2.0 %collective-permute-done.2.refs_4_ = bf16[2,8,8,128]{3,2,1,0:T(8,128)(2,1)S(1)} collective-permute-done((bf16[2,8,8,128]{3,2,1,0:T(8,128)(2,1)S(1)}, bf16[2,8,8,128]{3,2,1,0:T(8,128)(2,1)S(1)}, u32[]{:S(2)}, u32[]{:S(2)}) %collective-permute-start.2) | collective-permute-done | bytes 32800 | tf_op jit(solution)/shard_map/ppermute | solution.py:457
  11.8 0.0 copy-done.6
  11.8 0.0 copy-done.7
  11.8 4.7 %block.1 = (bf16[2,8,24,128]{3,2,1,0:T(8,128)(2,1)S(1)}, bf16[2,8,24,128]{3,2,1,0:T(8,128)(2,1)S(1)}, bf16[2,8,8,128]{3,2,1,0:T(8,128)(2,1)S(1)}, bf16[2,8,8,128...) custom-call(bf16[16,32,128]{2,1,0:T(8,128)(2,1)S(1)} %copy-done, ...), custom_call_target="tpu_custom_call" | custom-call | flops 1500000000 | bytes 2000000 | tf_op jit(solution)/shard_map/block/pallas_call | solution.py:529
  16.5 0.4 collective-permute-start.3
  16.9 1.1 %collective-permute-done.3.second_ref = bf16[896,128]{1,0:T(8,128)(2,1)S(1)} collective-permute-done((bf16[896,128]{1,0:T(8,128)(2,1)S(1)}, bf16[896,128]{1,0:T(8,128)(2,1)S(1)}, u32[]{:S(2)}, u32[]{:S(2)}) %collective-permute-start.3) | collective-permute-done | bytes 229408 | tf_op jit(solution)/shard_map/ppermute | solution.py:570
  18.0 0.1 pair.1
  18.1 13.5 %all_to_all.10.in_ref = bf16[16,56,128]{2,1,0:T(8,128)(2,1)S(1)} all-to-all(bf16[16,56,128]{2,1,0:T(8,128)(2,1)S(1)} %bitcast.10), channel_id=1, replica_groups={{0,1,2,3,4,5,6,7,16,17,18,19,20,21,22,23},{8,9,10,11,12,13,14,15,24,25,..., dimensions={0} | all-to-all | bytes 458752 | tf_op jit(solution)/shard_map/all_to_all | solution.py:568
  31.6 11.6 %all_to_all.11 = bf16[16,56,128]{2,1,0:T(8,128)(2,1)S(1)} all-to-all(bf16[16,56,128]{2,1,0:T(8,128)(2,1)S(1)} %add.1), channel_id=1, replica_groups={{0,1,2,3,4,5,6,7,16,17,18,19,20,21,22,23},{8,9,10,11,12,13,14,15,24,25,..., dimensions={0} | all-to-all | bytes 458752 | tf_op jit(solution)/shard_map/all_to_all | solution.py:568
  43.2 0.0 collective-permute-start.4
  43.2 1.4 %collective-permute-start.6 = (bf16[2,8,24,128]{3,2,1,0:T(8,128)(2,1)S(1)}, bf16[2,8,24,128]{3,2,1,0:T(8,128)(2,1)S(1)}, u32[]{:S(2)}, u32[]{:S(2)}) collective-permute-start(bf16[2,8,24,128]{3,2,1,0:T(8,128)(2,1)S(1)} %get-tuple-element.57), channel_id=1, source_target_pairs={{0,24},{1,25},{2,26},{3,27},{4,28},{5,29},{6,30},{7,31},{8,0},{9,1... | collective-permute-start | bytes 294920 | tf_op jit(solution)/shard_map/ppermute | solution.py:457
  44.6 0.7 %collective-permute-start.5 = (bf16[2,8,8,128]{3,2,1,0:T(8,128)(2,1)S(1)}, bf16[2,8,8,128]{3,2,1,0:T(8,128)(2,1)S(1)}, u32[]{:S(2)}, u32[]{:S(2)}) collective-permute-start(bf16[2,8,8,128]{3,2,1,0:T(8,128)(2,1)S(1)} %get-tuple-element.56), channel_id=1, source_target_pairs={{0,31},{1,24},{2,25},{3,26},{4,27},{5,28},{6,29},{7,30},{8,7},{9,0... | collective-permute-start | bytes 98312 | tf_op jit(solution)/shard_map/ppermute | solution.py:457
  45.4 1.6 %collective-permute-start.7 = (bf16[2,8,8,128]{3,2,1,0:T(8,128)(2,1)S(1)}, bf16[2,8,8,128]{3,2,1,0:T(8,128)(2,1)S(1)}, u32[]{:S(2)}, u32[]{:S(2)}) collective-permute-start(bf16[2,8,8,128]{3,2,1,0:T(8,128)(2,1)S(1)} %get-tuple-element.58), channel_id=1, source_target_pairs={{0,7},{1,0},{2,1},{3,2},{4,3},{5,4},{6,5},{7,6},{8,15},{9,8},{10,9... | collective-permute-start | bytes 98312 | tf_op jit(solution)/shard_map/ppermute | solution.py:457
  47.0 1.0 %collective-permute-done.5.diag_ref = bf16[2,8,8,128]{3,2,1,0:T(8,128)(2,1)S(1)} collective-permute-done((bf16[2,8,8,128]{3,2,1,0:T(8,128)(2,1)S(1)}, bf16[2,8,8,128]{3,2,1,0:T(8,128)(2,1)S(1)}, u32[]{:S(2)}, u32[]{:S(2)}) %collective-permute-start.5) | collective-permute-done | bytes 32800 | tf_op jit(solution)/shard_map/ppermute | solution.py:457
  48.0 1.6 %collective-permute-done.7.left_ref = bf16[2,8,8,128]{3,2,1,0:T(8,128)(2,1)S(1)} collective-permute-done((bf16[2,8,8,128]{3,2,1,0:T(8,128)(2,1)S(1)}, bf16[2,8,8,128]{3,2,1,0:T(8,128)(2,1)S(1)}, u32[]{:S(2)}, u32[]{:S(2)}) %collective-permute-start.7) | collective-permute-done | bytes 32800 | tf_op jit(solution)/shard_map/ppermute | solution.py:457
  49.6 0.0 collective-permute-done.6.above_ref
  49.6 0.0 collective-permute-done.4.other_ref
  49.6 1.0 %unpack.1 = (bf16[16,32,128]{2,1,0:T(8,128)(2,1)}, bf16[16,32,128]{2,1,0:T(8,128)(2,1)}, f32[1,128]{1,0:T(1,128)}, f32[128,384]{1,0:T(8,128)}, f32[128,128]{1,0:...) custom-call(bf16[896,128]{1,0:T(8,128)(2,1)S(1)} %bitcast.9, ...), custom_call_target="tpu_custom_call" | custom-call | tf_op jit(solution)/shard_map/unpack/pallas_call | solution.py:601
  (9 shorter events, 0.1 us)
Async XLA Ops:
  0.6 7.6 %copy-start = (bf16[16,32,128]{2,1,0:T(8,128)(2,1)S(1)}, bf16[16,32,128]{2,1,0:T(8,128)(2,1)}, u32[]{:S(2)}) copy-start(bf16[16,32,128]{2,1,0:T(8,128)(2,1)} %refs_0_.1) | copy-start | bytes 393220
  0.7 7.6 %copy-start.2 = (bf16[128,384]{1,0:T(8,128)(2,1)S(1)}, bf16[128,384]{1,0:T(8,128)(2,1)}, u32[]{:S(2)}) copy-start(bf16[128,384]{1,0:T(8,128)(2,1)} %refs_7_.1) | copy-start | bytes 294916
  0.7 7.6 %copy-start.3 = (f32[128]{0:T(128)S(1)}, f32[128]{0:T(128)}, u32[]{:S(2)}) copy-start(f32[128]{0:T(128)} %param.10) | copy-start | bytes 1540
  1.7 6.5 %collective-permute-start = (bf16[2,8,24,128]{3,2,1,0:T(8,128)(2,1)S(1)}, bf16[2,8,24,128]{3,2,1,0:T(8,128)(2,1)S(1)}, u32[]{:S(2)}, u32[]{:S(2)}) collective-permute-start(bf16[2,8,24,128]{3,2,1,0:T(8,128)(2,1)S(1)} %get-tuple-element.39), channel_id=1, source_target_pairs={{0,8},{1,9},{2,10},{3,11},{4,12},{5,13},{6,14},{7,15},{8,16},{9,17... | collective-permute-start | bytes 294920 | tf_op jit(solution)/shard_map/ppermute | solution.py:457
  2.3 7.5 %collective-permute-start.1 = (bf16[2,8,8,128]{3,2,1,0:T(8,128)(2,1)S(1)}, bf16[2,8,8,128]{3,2,1,0:T(8,128)(2,1)S(1)}, u32[]{:S(2)}, u32[]{:S(2)}) collective-permute-start(bf16[2,8,8,128]{3,2,1,0:T(8,128)(2,1)S(1)} %get-tuple-element.40), channel_id=1, source_target_pairs={{0,1},{1,2},{2,3},{3,4},{4,5},{5,6},{6,7},{7,0},{8,9},{9,10},{10,1... | collective-permute-start | bytes 98312 | tf_op jit(solution)/shard_map/ppermute | solution.py:457
  4.8 6.9 %collective-permute-start.2 = (bf16[2,8,8,128]{3,2,1,0:T(8,128)(2,1)S(1)}, bf16[2,8,8,128]{3,2,1,0:T(8,128)(2,1)S(1)}, u32[]{:S(2)}, u32[]{:S(2)}) collective-permute-start(bf16[2,8,8,128]{3,2,1,0:T(8,128)(2,1)S(1)} %get-tuple-element.41), channel_id=1, source_target_pairs={{0,9},{1,10},{2,11},{3,12},{4,13},{5,14},{6,15},{7,8},{8,17},{9,18... | collective-permute-start | bytes 98312 | tf_op jit(solution)/shard_map/ppermute | solution.py:457
  7.2 4.6 %copy-start.1 = (bf16[16,32,128]{2,1,0:T(8,128)(2,1)S(1)}, bf16[16,32,128]{2,1,0:T(8,128)(2,1)}, u32[]{:S(2)}) copy-start(bf16[16,32,128]{2,1,0:T(8,128)(2,1)} %refs_1_.1) | copy-start | bytes 393220
  7.2 4.6 %copy-start.4 = (bf16[128,512]{1,0:T(8,128)(2,1)S(1)}, bf16[128,512]{1,0:T(8,128)(2,1)}, u32[]{:S(2)}) copy-start(bf16[128,512]{1,0:T(8,128)(2,1)} %refs_10_.1) | copy-start | bytes 393220
  7.2 4.6 %copy-start.5 = (bf16[512,128]{1,0:T(8,128)(2,1)S(1)}, bf16[512,128]{1,0:T(8,128)(2,1)}, u32[]{:S(2)}) copy-start(bf16[512,128]{1,0:T(8,128)(2,1)} %refs_11_.1) | copy-start | bytes 393220
  7.2 4.6 %copy-start.6 = (bf16[128,128]{1,0:T(8,128)(2,1)S(1)}, bf16[128,128]{1,0:T(8,128)(2,1)}, u32[]{:S(2)}) copy-start(bf16[128,128]{1,0:T(8,128)(2,1)} %refs_8_.1) | copy-start | bytes 98308
  7.2 4.6 %copy-start.7 = (f32[128]{0:T(128)S(1)}, f32[128]{0:T(128)}, u32[]{:S(2)}) copy-start(f32[128]{0:T(128)} %param.14) | copy-start | bytes 1540
  16.5 1.6 %collective-permute-start.3 = (bf16[896,128]{1,0:T(8,128)(2,1)S(1)}, bf16[896,128]{1,0:T(8,128)(2,1)S(1)}, u32[]{:S(2)}, u32[]{:S(2)}) collective-permute-start(bf16[896,128]{1,0:T(8,128)(2,1)S(1)} %get-tuple-element.55), channel_id=1, source_target_pairs={{0,8},{1,9},{2,10},{3,11},{4,12},{5,13},{6,14},{7,15},{8,0},{9,1},... | collective-permute-start | bytes 688136 | tf_op jit(solution)/shard_map/ppermute | solution.py:570
  43.2 6.4 %collective-permute-start.4 = (bf16[896,128]{1,0:T(8,128)(2,1)S(1)}, bf16[896,128]{1,0:T(8,128)(2,1)S(1)}, u32[]{:S(2)}, u32[]{:S(2)}) collective-permute-start(bf16[896,128]{1,0:T(8,128)(2,1)S(1)} %bitcast.8), channel_id=1, source_target_pairs={{0,8},{1,9},{2,10},{3,11},{4,12},{5,13},{6,14},{7,15},{8,0},{9,1},... | collective-permute-start | bytes 688136 | tf_op jit(solution)/shard_map/ppermute | solution.py:588
  43.2 6.4 %collective-permute-start.6 = (bf16[2,8,24,128]{3,2,1,0:T(8,128)(2,1)S(1)}, bf16[2,8,24,128]{3,2,1,0:T(8,128)(2,1)S(1)}, u32[]{:S(2)}, u32[]{:S(2)}) collective-permute-start(bf16[2,8,24,128]{3,2,1,0:T(8,128)(2,1)S(1)} %get-tuple-element.57), channel_id=1, source_target_pairs={{0,24},{1,25},{2,26},{3,27},{4,28},{5,29},{6,30},{7,31},{8,0},{9,1... | collective-permute-start | bytes 294920 | tf_op jit(solution)/shard_map/ppermute | solution.py:457
  44.6 3.3 %collective-permute-start.5 = (bf16[2,8,8,128]{3,2,1,0:T(8,128)(2,1)S(1)}, bf16[2,8,8,128]{3,2,1,0:T(8,128)(2,1)S(1)}, u32[]{:S(2)}, u32[]{:S(2)}) collective-permute-start(bf16[2,8,8,128]{3,2,1,0:T(8,128)(2,1)S(1)} %get-tuple-element.56), channel_id=1, source_target_pairs={{0,31},{1,24},{2,25},{3,26},{4,27},{5,28},{6,29},{7,30},{8,7},{9,0... | collective-permute-start | bytes 98312 | tf_op jit(solution)/shard_map/ppermute | solution.py:457
  45.4 4.2 %collective-permute-start.7 = (bf16[2,8,8,128]{3,2,1,0:T(8,128)(2,1)S(1)}, bf16[2,8,8,128]{3,2,1,0:T(8,128)(2,1)S(1)}, u32[]{:S(2)}, u32[]{:S(2)}) collective-permute-start(bf16[2,8,8,128]{3,2,1,0:T(8,128)(2,1)S(1)} %get-tuple-element.58), channel_id=1, source_target_pairs={{0,7},{1,0},{2,1},{3,2},{4,3},{5,4},{6,5},{7,6},{8,15},{9,8},{10,9... | collective-permute-start | bytes 98312 | tf_op jit(solution)/shard_map/ppermute | solution.py:457

commit v2 on v1

--- a/solution.py
+++ b/solution.py
@@ -393,12 +393,6 @@
     factor,
     mine_ref,
     other_ref,
-    diag_ref,
-    above_ref,
-    left_ref,
-    own_ref,
-    out_ref,
-    grad_ref,
     gain1_ref,
     qkv_ref,
     proj_ref,
@@ -410,14 +404,6 @@
 ):
     width, hidden_units = fc1_ref.shape
     half = mine_ref.shape[0]
-    early = own_ref.shape[2] - SHIFT
-    cuts = ((slice(0, SHIFT), slice(early, None)), (slice(SHIFT, SHIFT + early), slice(0, early)))
-    for index, target in enumerate((out_ref, grad_ref)):
-        for cols, source in cuts:
-            target[:SHIFT, cols, :] = own_ref[index, :, source, :]
-            target[SHIFT:, cols, :] = above_ref[index, :, source, :]
-        target[:SHIFT, SHIFT + early :, :] = left_ref[index]
-        target[SHIFT:, SHIFT + early :, :] = diag_ref[index]
     core = lax.axis_index("group") % 2
     summed_ref[pl.ds(pl.multiple_of(core * half, 16), half), :] = mine_ref[...]
     summed_ref[pl.ds(pl.multiple_of((1 - core) * half, 16), half), :] = other_ref[...]
@@ -441,6 +427,17 @@
     gains = rows(start, 16)
     gain1_ref[...] = gains[0:1]
     gain2_ref[...] = gains[1:2]
+
+
+def tiles_kernel(diag_ref, above_ref, left_ref, own_ref, out_ref, grad_ref):
+    early = own_ref.shape[2] - SHIFT
+    cuts = ((slice(0, SHIFT), slice(early, None)), (slice(SHIFT, SHIFT + early), slice(0, early)))
+    for index, target in enumerate((out_ref, grad_ref)):
+        for cols, source in cuts:
+            target[:SHIFT, cols, :] = own_ref[index, :, source, :]
+            target[SHIFT:, cols, :] = above_ref[index, :, source, :]
+        target[:SHIFT, SHIFT + early :, :] = left_ref[index]
+        target[SHIFT:, SHIFT + early :, :] = diag_ref[index]
 
 
 def neighbour_pairs(row_step, col_step):
@@ -588,9 +585,16 @@
     other = lax.ppermute(mine, AXES, pairs)
 
     factor = 1.0 / math.sqrt(row_count * groups * col_count * tiles)
+    block_output, grad_tokens = pl.pallas_call(
+        tiles_kernel,
+        out_shape=(array(tokens.shape), array(tokens.shape)),
+        in_specs=[vmem] * 4,
+        out_specs=(vmem,) * 2,
+        name="tiles",
+        compiler_params=PARAMS,
+        cost_estimate=pl.CostEstimate(flops=4_000_000, bytes_accessed=600_000, transcendentals=0),
+    )(back_diag, back_below, back_right, own_out)
     (
-        block_output,
-        grad_tokens,
         grad_gain1,
         grad_qkv,
         grad_proj,
@@ -601,8 +605,6 @@
     ) = pl.pallas_call(
         functools.partial(unpack_kernel, heads, factor),
         out_shape=(
-            array(tokens.shape),
-            array(tokens.shape),
             jax.ShapeDtypeStruct((1, width), F32),
             jax.ShapeDtypeStruct(w_qkv.shape, F32),
             jax.ShapeDtypeStruct(w_proj.shape, F32),
@@ -611,12 +613,12 @@
             jax.ShapeDtypeStruct(w_fc1.shape, F32),
             jax.ShapeDtypeStruct(w_fc2.shape, F32),
         ),
-        in_specs=[vmem] * 6,
-        out_specs=(vmem,) * 9,
+        in_specs=[vmem] * 2,
+        out_specs=(vmem,) * 7,
         scratch_shapes=[pltpu.VMEM((2 * half, width), BF16)],
         name="unpack",
         compiler_params=PARAMS,
-    )(mine, other, back_diag, back_below, back_right, own_out)
+    )(mine, other)
 
     return (
         block_output,

time: 50.9 us -> 51.5 us (1.012)
  Pallas kernels: 8.77 us -> 9.44 us
    pallas_call x0 -> x1, Pallas kernels: none -> 0.73 us  [shards(): pl.pallas_call(tiles_kernel, out_shape=(array(tokens.shape), array(tokens...]
  transfers between devices with their start and end apart: 8 -> 8, of which waited for: 5 -> 5; matrix products, arithmetic and copies ran while one was open for 0% -> 0% of each run, Pallas kernels for 4% -> 5%
where the time goes in v2:
time: 51.5 us; the launch traced here: 51.3 us
  blocking collectives  25.1 us (49%)
  starting transfers between devices  9.73 us (19%)
  Pallas kernels  9.44 us (18%)
  waiting for transfers between devices  6.29 us (12%)
  between operations  0.77 us (1%)
    all_to_all x2, blocking collectives, exchanged(): lax.all_to_all(value, AXES, 0, 0, tiled=True, axis_index_groups=same_core)  25.1 us
    ppermute x6, starting transfers between devices, passed_along(): return lax.ppermute(value, AXES, neighbour_pairs(row_step, col_step))  9.3 us
    ppermute x6, waiting for transfers between devices, passed_along(): return lax.ppermute(value, AXES, neighbour_pairs(row_step, col_step))  5.16 us
    pallas_call x1, Pallas kernels, shards(): pl.pallas_call(functools.partial(block_kernel, heads, windows), out_shape...  4.67 us
    ppermute x1, waiting for transfers between devices, shards(): received = lax.ppermute(sent, AXES, pairs)  1.13 us
    pallas_call x1, Pallas kernels, shards(): pl.pallas_call(cut_kernel, out_shape=(array((2, SHIFT, keep, width)), arr...  1.04 us
  transfers between devices with their start and end apart: 8, of which 5 were waited for; matrix products, arithmetic and copies ran while one was open for 0% of the time, Pallas kernels for 5%

profile of v2, /device:TPU:0, one launch (start us, length us, event | category | flops | bytes accessed | tf_op | source)
XLA Modules:
  0.0 51.3 jit_solution(11472948001066461331)
XLA Ops:
  0.6 0.0 copy-start
  0.7 0.0 copy-start.2
  0.7 0.0 copy-start.3
  0.7 1.0 %cut.1 = (bf16[2,8,24,128]{3,2,1,0:T(8,128)(2,1)S(1)}, bf16[2,8,8,128]{3,2,1,0:T(8,128)(2,1)S(1)}, bf16[2,8,8,128]{3,2,1,0:T(8,128)(2,1)S(1)}, f32[31,4,31]{2,1,0:T(4,128)S(1)}) custom-call(bf16[16,32,128]{2,1,0:T(8,128)(2,1)} %refs_0_.1, bf16[16,32,128]{2,1,0:T(8,128)(2,1)} %refs_1_.1, f32[31,4,31]{2,1,0:T(4,128)} %bitcast.14), custom_call_target="tpu_custom_call" | custom-call | tf_op jit(solution)/shard_map/cut/pallas_call | solution.py:474
  1.7 0.5 %collective-permute-start = (bf16[2,8,24,128]{3,2,1,0:T(8,128)(2,1)S(1)}, bf16[2,8,24,128]{3,2,1,0:T(8,128)(2,1)S(1)}, u32[]{:S(2)}, u32[]{:S(2)}) collective-permute-start(bf16[2,8,24,128]{3,2,1,0:T(8,128)(2,1)S(1)} %get-tuple-element.39), channel_id=1, source_target_pairs={{0,8},{1,9},{2,10},{3,11},{4,12},{5,13},{6,14},{7,15},{8,16},{9,17... | collective-permute-start | bytes 294920 | tf_op jit(solution)/shard_map/ppermute | solution.py:454
  2.3 2.6 %collective-permute-start.1 = (bf16[2,8,8,128]{3,2,1,0:T(8,128)(2,1)S(1)}, bf16[2,8,8,128]{3,2,1,0:T(8,128)(2,1)S(1)}, u32[]{:S(2)}, u32[]{:S(2)}) collective-permute-start(bf16[2,8,8,128]{3,2,1,0:T(8,128)(2,1)S(1)} %get-tuple-element.40), channel_id=1, source_target_pairs={{0,1},{1,2},{2,3},{3,4},{4,5},{5,6},{6,7},{7,0},{8,9},{9,10},{10,1... | collective-permute-start | bytes 98312 | tf_op jit(solution)/shard_map/ppermute | solution.py:454
  4.8 2.4 %collective-permute-start.2 = (bf16[2,8,8,128]{3,2,1,0:T(8,128)(2,1)S(1)}, bf16[2,8,8,128]{3,2,1,0:T(8,128)(2,1)S(1)}, u32[]{:S(2)}, u32[]{:S(2)}) collective-permute-start(bf16[2,8,8,128]{3,2,1,0:T(8,128)(2,1)S(1)} %get-tuple-element.41), channel_id=1, source_target_pairs={{0,9},{1,10},{2,11},{3,12},{4,13},{5,14},{6,15},{7,8},{8,17},{9,18... | collective-permute-start | bytes 98312 | tf_op jit(solution)/shard_map/ppermute | solution.py:454
  7.2 0.0 copy-start.7
  7.2 0.9 %bias.1.bias_ref.refs_5_ = f32[2,1024,256]{2,1,0:T(8,128)S(1)} custom-call(f32[31,4,31]{2,1,0:T(4,128)S(1)} %get-tuple-element.42.table_ref), custom_call_target="tpu_custom_call" | custom-call | flops 8000000 | bytes 2000000 | tf_op jit(solution)/shard_map/bias/pallas_call | solution.py:492
  8.2 0.0 collective-permute-done.below_ref.refs_2_
  8.2 0.0 copy-done
  8.2 1.0 %early.1 = (f32[256,128]{1,0:T(8,128)S(1)}, bf16[256,128]{1,0:T(8,128)(2,1)S(1)}, f32[256,128]{1,0:T(8,128)S(1)}, f32[256,1]{1,0:T(8,128)S(1)}, f32[256,128]{1,0...) custom-call(bf16[16,32,128]{2,1,0:T(8,128)(2,1)S(1)} %copy-done, ...), custom_call_target="tpu_custom_call" | custom-call | flops 500000000 | bytes 2000000 | tf_op jit(solution)/shard_map/early/pallas_call | solution.py:514
  9.2 0.5 %collective-permute-done.1.refs_3_ = bf16[2,8,8,128]{3,2,1,0:T(8,128)(2,1)S(1)} collective-permute-done((bf16[2,8,8,128]{3,2,1,0:T(8,128)(2,1)S(1)}, bf16[2,8,8,128]{3,2,1,0:T(8,128)(2,1)S(1)}, u32[]{:S(2)}, u32[]{:S(2)}) %collective-permute-start.1) | collective-permute-done | bytes 32800 | tf_op jit(solution)/shard_map/ppermute | solution.py:454
  9.8 2.0 %collective-permute-done.2.refs_4_ = bf16[2,8,8,128]{3,2,1,0:T(8,128)(2,1)S(1)} collective-permute-done((bf16[2,8,8,128]{3,2,1,0:T(8,128)(2,1)S(1)}, bf16[2,8,8,128]{3,2,1,0:T(8,128)(2,1)S(1)}, u32[]{:S(2)}, u32[]{:S(2)}) %collective-permute-start.2) | collective-permute-done | bytes 32800 | tf_op jit(solution)/shard_map/ppermute | solution.py:454
  11.8 0.0 copy-done.6
  11.8 0.0 copy-done.7
  11.8 4.7 %block.1 = (bf16[2,8,24,128]{3,2,1,0:T(8,128)(2,1)S(1)}, bf16[2,8,24,128]{3,2,1,0:T(8,128)(2,1)S(1)}, bf16[2,8,8,128]{3,2,1,0:T(8,128)(2,1)S(1)}, bf16[2,8,8,128...) custom-call(bf16[16,32,128]{2,1,0:T(8,128)(2,1)S(1)} %copy-done, ...), custom_call_target="tpu_custom_call" | custom-call | flops 1500000000 | bytes 2000000 | tf_op jit(solution)/shard_map/block/pallas_call | solution.py:526
  16.5 0.4 collective-permute-start.6
  16.9 1.1 %collective-permute-done.6.second_ref = bf16[896,128]{1,0:T(8,128)(2,1)S(1)} collective-permute-done((bf16[896,128]{1,0:T(8,128)(2,1)S(1)}, bf16[896,128]{1,0:T(8,128)(2,1)S(1)}, u32[]{:S(2)}, u32[]{:S(2)}) %collective-permute-start.6) | collective-permute-done | bytes 229408 | tf_op jit(solution)/shard_map/ppermute | solution.py:567
  18.0 0.1 pair.1
  18.1 13.5 %all_to_all.10.in_ref = bf16[16,56,128]{2,1,0:T(8,128)(2,1)S(1)} all-to-all(bf16[16,56,128]{2,1,0:T(8,128)(2,1)S(1)} %bitcast.10), channel_id=1, replica_groups={{0,1,2,3,4,5,6,7,16,17,18,19,20,21,22,23},{8,9,10,11,12,13,14,15,24,25,..., dimensions={0} | all-to-all | bytes 458752 | tf_op jit(solution)/shard_map/all_to_all | solution.py:565
  31.6 11.6 %all_to_all.11 = bf16[16,56,128]{2,1,0:T(8,128)(2,1)S(1)} all-to-all(bf16[16,56,128]{2,1,0:T(8,128)(2,1)S(1)} %add.1), channel_id=1, replica_groups={{0,1,2,3,4,5,6,7,16,17,18,19,20,21,22,23},{8,9,10,11,12,13,14,15,24,25,..., dimensions={0} | all-to-all | bytes 458752 | tf_op jit(solution)/shard_map/all_to_all | solution.py:565
  43.2 0.0 collective-permute-start.7
  43.2 1.4 %collective-permute-start.4 = (bf16[2,8,24,128]{3,2,1,0:T(8,128)(2,1)S(1)}, bf16[2,8,24,128]{3,2,1,0:T(8,128)(2,1)S(1)}, u32[]{:S(2)}, u32[]{:S(2)}) collective-permute-start(bf16[2,8,24,128]{3,2,1,0:T(8,128)(2,1)S(1)} %get-tuple-element.55), channel_id=1, source_target_pairs={{0,24},{1,25},{2,26},{3,27},{4,28},{5,29},{6,30},{7,31},{8,0},{9,1... | collective-permute-start | bytes 294920 | tf_op jit(solution)/shard_map/ppermute | solution.py:454
  44.6 0.7 %collective-permute-start.3 = (bf16[2,8,8,128]{3,2,1,0:T(8,128)(2,1)S(1)}, bf16[2,8,8,128]{3,2,1,0:T(8,128)(2,1)S(1)}, u32[]{:S(2)}, u32[]{:S(2)}) collective-permute-start(bf16[2,8,8,128]{3,2,1,0:T(8,128)(2,1)S(1)} %get-tuple-element.54), channel_id=1, source_target_pairs={{0,31},{1,24},{2,25},{3,26},{4,27},{5,28},{6,29},{7,30},{8,7},{9,0... | collective-permute-start | bytes 98312 | tf_op jit(solution)/shard_map/ppermute | solution.py:454
  45.4 1.6 %collective-permute-start.5 = (bf16[2,8,8,128]{3,2,1,0:T(8,128)(2,1)S(1)}, bf16[2,8,8,128]{3,2,1,0:T(8,128)(2,1)S(1)}, u32[]{:S(2)}, u32[]{:S(2)}) collective-permute-start(bf16[2,8,8,128]{3,2,1,0:T(8,128)(2,1)S(1)} %get-tuple-element.56), channel_id=1, source_target_pairs={{0,7},{1,0},{2,1},{3,2},{4,3},{5,4},{6,5},{7,6},{8,15},{9,8},{10,9... | collective-permute-start | bytes 98312 | tf_op jit(solution)/shard_map/ppermute | solution.py:454
  47.0 1.0 %collective-permute-done.3.diag_ref = bf16[2,8,8,128]{3,2,1,0:T(8,128)(2,1)S(1)} collective-permute-done((bf16[2,8,8,128]{3,2,1,0:T(8,128)(2,1)S(1)}, bf16[2,8,8,128]{3,2,1,0:T(8,128)(2,1)S(1)}, u32[]{:S(2)}, u32[]{:S(2)}) %collective-permute-start.3) | collective-permute-done | bytes 32800 | tf_op jit(solution)/shard_map/ppermute | solution.py:454
  48.0 1.6 %collective-permute-done.5.left_ref = bf16[2,8,8,128]{3,2,1,0:T(8,128)(2,1)S(1)} collective-permute-done((bf16[2,8,8,128]{3,2,1,0:T(8,128)(2,1)S(1)}, bf16[2,8,8,128]{3,2,1,0:T(8,128)(2,1)S(1)}, u32[]{:S(2)}, u32[]{:S(2)}) %collective-permute-start.5) | collective-permute-done | bytes 32800 | tf_op jit(solution)/shard_map/ppermute | solution.py:454
  49.6 0.0 collective-permute-done.4.above_ref
  49.6 0.7 %tiles.1 = (bf16[16,32,128]{2,1,0:T(8,128)(2,1)}, bf16[16,32,128]{2,1,0:T(8,128)(2,1)}) custom-call(bf16[2,8,8,128]{3,2,1,0:T(8,128)(2,1)S(1)} %collective-permute-done.3.diag_ref, bf16[2,8,24,128]{3,2,1,0:T(8,128)(2,1)S(1)} %collective-permute-done.4.above_ref, bf16[2,8,8,128]{3,2,1,0:T(8,128)(2,1)S(1)} %collective-permute-done.5.left_ref, ...), custom_call_target="tpu_custom_call" | custom-call | flops 4000000 | bytes 600000 | tf_op jit(solution)/shard_map/tiles/pallas_call | solution.py:588
  50.4 0.0 collective-permute-done.7.other_ref
  50.4 1.0 %unpack.1 = (f32[1,128]{1,0:T(1,128)}, f32[128,384]{1,0:T(8,128)}, f32[128,128]{1,0:T(8,128)}, f32[31,4,31]{2,1,0:T(4,128)}, f32[1,128]{1,0:T(1,128)}, /*index=5*/f32[128,512]{1,0:T(8,128)}, f32[512,128]{1,0:T(8,128)}) custom-call(bf16[896,128]{1,0:T(8,128)(2,1)S(1)} %bitcast.9, bf16[896,128]{1,0:T(8,128)(2,1)S(1)} %collective-permute-done.7.other_ref), custom_call_target="tpu_custom_call" | custom-call | tf_op jit(solution)/shard_map/unpack/pallas_call | solution.py:605
  (10 shorter events, 0.1 us)
Async XLA Ops:
  0.6 7.6 %copy-start = (bf16[16,32,128]{2,1,0:T(8,128)(2,1)S(1)}, bf16[16,32,128]{2,1,0:T(8,128)(2,1)}, u32[]{:S(2)}) copy-start(bf16[16,32,128]{2,1,0:T(8,128)(2,1)} %refs_0_.1) | copy-start | bytes 393220
  0.7 7.6 %copy-start.2 = (bf16[128,384]{1,0:T(8,128)(2,1)S(1)}, bf16[128,384]{1,0:T(8,128)(2,1)}, u32[]{:S(2)}) copy-start(bf16[128,384]{1,0:T(8,128)(2,1)} %refs_7_.1) | copy-start | bytes 294916
  0.7 7.6 %copy-start.3 = (f32[128]{0:T(128)S(1)}, f32[128]{0:T(128)}, u32[]{:S(2)}) copy-start(f32[128]{0:T(128)} %param.10) | copy-start | bytes 1540
  1.7 6.5 %collective-permute-start = (bf16[2,8,24,128]{3,2,1,0:T(8,128)(2,1)S(1)}, bf16[2,8,24,128]{3,2,1,0:T(8,128)(2,1)S(1)}, u32[]{:S(2)}, u32[]{:S(2)}) collective-permute-start(bf16[2,8,24,128]{3,2,1,0:T(8,128)(2,1)S(1)} %get-tuple-element.39), channel_id=1, source_target_pairs={{0,8},{1,9},{2,10},{3,11},{4,12},{5,13},{6,14},{7,15},{8,16},{9,17... | collective-permute-start | bytes 294920 | tf_op jit(solution)/shard_map/ppermute | solution.py:454
  2.3 7.5 %collective-permute-start.1 = (bf16[2,8,8,128]{3,2,1,0:T(8,128)(2,1)S(1)}, bf16[2,8,8,128]{3,2,1,0:T(8,128)(2,1)S(1)}, u32[]{:S(2)}, u32[]{:S(2)}) collective-permute-start(bf16[2,8,8,128]{3,2,1,0:T(8,128)(2,1)S(1)} %get-tuple-element.40), channel_id=1, source_target_pairs={{0,1},{1,2},{2,3},{3,4},{4,5},{5,6},{6,7},{7,0},{8,9},{9,10},{10,1... | collective-permute-start | bytes 98312 | tf_op jit(solution)/shard_map/ppermute | solution.py:454
  4.8 6.9 %collective-permute-start.2 = (bf16[2,8,8,128]{3,2,1,0:T(8,128)(2,1)S(1)}, bf16[2,8,8,128]{3,2,1,0:T(8,128)(2,1)S(1)}, u32[]{:S(2)}, u32[]{:S(2)}) collective-permute-start(bf16[2,8,8,128]{3,2,1,0:T(8,128)(2,1)S(1)} %get-tuple-element.41), channel_id=1, source_target_pairs={{0,9},{1,10},{2,11},{3,12},{4,13},{5,14},{6,15},{7,8},{8,17},{9,18... | collective-permute-start | bytes 98312 | tf_op jit(solution)/shard_map/ppermute | solution.py:454
  7.2 4.6 %copy-start.1 = (bf16[16,32,128]{2,1,0:T(8,128)(2,1)S(1)}, bf16[16,32,128]{2,1,0:T(8,128)(2,1)}, u32[]{:S(2)}) copy-start(bf16[16,32,128]{2,1,0:T(8,128)(2,1)} %refs_1_.1) | copy-start | bytes 393220
  7.2 4.6 %copy-start.4 = (bf16[128,512]{1,0:T(8,128)(2,1)S(1)}, bf16[128,512]{1,0:T(8,128)(2,1)}, u32[]{:S(2)}) copy-start(bf16[128,512]{1,0:T(8,128)(2,1)} %refs_10_.1) | copy-start | bytes 393220
  7.2 4.6 %copy-start.5 = (bf16[512,128]{1,0:T(8,128)(2,1)S(1)}, bf16[512,128]{1,0:T(8,128)(2,1)}, u32[]{:S(2)}) copy-start(bf16[512,128]{1,0:T(8,128)(2,1)} %refs_11_.1) | copy-start | bytes 393220
  7.2 4.6 %copy-start.6 = (bf16[128,128]{1,0:T(8,128)(2,1)S(1)}, bf16[128,128]{1,0:T(8,128)(2,1)}, u32[]{:S(2)}) copy-start(bf16[128,128]{1,0:T(8,128)(2,1)} %refs_8_.1) | copy-start | bytes 98308
  7.2 4.6 %copy-start.7 = (f32[128]{0:T(128)S(1)}, f32[128]{0:T(128)}, u32[]{:S(2)}) copy-start(f32[128]{0:T(128)} %param.14) | copy-start | bytes 1540
  16.5 1.6 %collective-permute-start.6 = (bf16[896,128]{1,0:T(8,128)(2,1)S(1)}, bf16[896,128]{1,0:T(8,128)(2,1)S(1)}, u32[]{:S(2)}, u32[]{:S(2)}) collective-permute-start(bf16[896,128]{1,0:T(8,128)(2,1)S(1)} %get-tuple-element.61), channel_id=1, source_target_pairs={{0,8},{1,9},{2,10},{3,11},{4,12},{5,13},{6,14},{7,15},{8,0},{9,1},... | collective-permute-start | bytes 688136 | tf_op jit(solution)/shard_map/ppermute | solution.py:567
  43.2 7.2 %collective-permute-start.7 = (bf16[896,128]{1,0:T(8,128)(2,1)S(1)}, bf16[896,128]{1,0:T(8,128)(2,1)S(1)}, u32[]{:S(2)}, u32[]{:S(2)}) collective-permute-start(bf16[896,128]{1,0:T(8,128)(2,1)S(1)} %bitcast.8), channel_id=1, source_target_pairs={{0,8},{1,9},{2,10},{3,11},{4,12},{5,13},{6,14},{7,15},{8,0},{9,1},... | collective-permute-start | bytes 688136 | tf_op jit(solution)/shard_map/ppermute | solution.py:585
  43.2 6.4 %collective-permute-start.4 = (bf16[2,8,24,128]{3,2,1,0:T(8,128)(2,1)S(1)}, bf16[2,8,24,128]{3,2,1,0:T(8,128)(2,1)S(1)}, u32[]{:S(2)}, u32[]{:S(2)}) collective-permute-start(bf16[2,8,24,128]{3,2,1,0:T(8,128)(2,1)S(1)} %get-tuple-element.55), channel_id=1, source_target_pairs={{0,24},{1,25},{2,26},{3,27},{4,28},{5,29},{6,30},{7,31},{8,0},{9,1... | collective-permute-start | bytes 294920 | tf_op jit(solution)/shard_map/ppermute | solution.py:454
  44.6 3.3 %collective-permute-start.3 = (bf16[2,8,8,128]{3,2,1,0:T(8,128)(2,1)S(1)}, bf16[2,8,8,128]{3,2,1,0:T(8,128)(2,1)S(1)}, u32[]{:S(2)}, u32[]{:S(2)}) collective-permute-start(bf16[2,8,8,128]{3,2,1,0:T(8,128)(2,1)S(1)} %get-tuple-element.54), channel_id=1, source_target_pairs={{0,31},{1,24},{2,25},{3,26},{4,27},{5,28},{6,29},{7,30},{8,7},{9,0... | collective-permute-start | bytes 98312 | tf_op jit(solution)/shard_map/ppermute | solution.py:454
  45.4 4.2 %collective-permute-start.5 = (bf16[2,8,8,128]{3,2,1,0:T(8,128)(2,1)S(1)}, bf16[2,8,8,128]{3,2,1,0:T(8,128)(2,1)S(1)}, u32[]{:S(2)}, u32[]{:S(2)}) collective-permute-start(bf16[2,8,8,128]{3,2,1,0:T(8,128)(2,1)S(1)} %get-tuple-element.56), channel_id=1, source_target_pairs={{0,7},{1,0},{2,1},{3,2},{4,3},{5,4},{6,5},{7,6},{8,15},{9,8},{10,9... | collective-permute-start | bytes 98312 | tf_op jit(solution)/shard_map/ppermute | solution.py:454
